TPU v7x, 32 devices: a whole 2x2x4 slice. The times are simulated.
32 devices in a mesh: data: 4 (over x, y), tp: 8 (over z, core).
Axes of the slice: x: 2, y: 2, z: 4, core: 2. Of those that a mesh axis runs over, the one named last changes fastest.
Arguments:
- X: bfloat16 [16384, 1280], P(('data', 'tp')), parts along dimension 0
- gamma: float32 [1280], replicated
- W1: bfloat16 [1280, 5120], P(None, 'tp')
- W2: bfloat16 [5120, 1280], P('tp')
- dY: bfloat16 [16384, 1280], P(('data', 'tp')), parts along dimension 0
Outputs:
- output 1: bfloat16 [16384, 1280], P(('data', 'tp')), parts along dimension 0
- output 2: bfloat16 [16384, 1280], P(('data', 'tp')), parts along dimension 0
- output 3: float32 [5120, 5120], P('data', 'tp'), parts along dimension 0
- output 4: float32 [20480, 1280], P(('data', 'tp')), parts along dimension 0
- output 5: float32 [5120], P('data'), parts along dimension 0
There are 4 independent parts. A program takes and returns all parts, laid end to end along the dimension named above; an argument that names none is the same for every part.
All inputs are finite; a program needn't handle non-finite values.
Results may differ from a plain program's by a relative error of at most 0.001.
Values are sent between devices in bfloat16 or wider.
A program may use at most 1 GiB of HBM per device.

v0:
```python
import jax
import jax.numpy as jnp
from jax import lax
from jax.sharding import PartitionSpec as P

EPS = 1e-6


def _gelu(a):
    return jax.nn.gelu(a, approximate=True)


def _ln(x):
    mu = jnp.mean(x, axis=-1, keepdims=True)
    xc = x - mu
    var = jnp.mean(xc * xc, axis=-1, keepdims=True)
    rstd = lax.rsqrt(var + EPS)
    return xc * rstd, rstd


def _tn(a, b):
    return lax.dot_general(a, b, (((0,), (0,)), ((), ())), preferred_element_type=jnp.float32)


def _nt(a, b):
    return lax.dot_general(a, b, (((1,), (1,)), ((), ())), preferred_element_type=jnp.float32)


def solution(mesh):
    rows = P(("data", "tp"), None)

    def body(X, gamma, W1, W2, dY):
        x = X.astype(jnp.float32)
        xhatv, rstd = _ln(x)
        Xn = lax.all_gather((xhatv * gamma).astype(jnp.bfloat16), "tp", axis=0, tiled=True)
        A = jnp.dot(Xn, W1, preferred_element_type=jnp.float32)
        H = _gelu(A).astype(jnp.bfloat16)
        Yp = jnp.dot(H, W2, preferred_element_type=jnp.float32)
        Y = (x + lax.psum_scatter(Yp, "tp", scatter_dimension=0, tiled=True)).astype(jnp.bfloat16)
        g = lax.all_gather(dY, "tp", axis=0, tiled=True)
        dW2 = _tn(H, g)
        dH = _nt(g, W2)
        dA = jax.vjp(_gelu, A)[1](dH)[0].astype(jnp.bfloat16)
        dW1 = _tn(Xn, dA)
        dXn = lax.psum_scatter(_nt(dA, W1), "tp", scatter_dimension=0, tiled=True)
        dgamma = lax.psum(jnp.sum(dXn * xhatv, axis=0), "tp")
        dxhat = dXn * gamma
        dx = rstd * (dxhat - jnp.mean(dxhat, axis=-1, keepdims=True) - xhatv * jnp.mean(dxhat * xhatv, axis=-1, keepdims=True))
        dX = (dY.astype(jnp.float32) + dx).astype(jnp.bfloat16)
        return Y, dX, dW1, dW2, dgamma

    return jax.shard_map(body, mesh=mesh,
                         in_specs=(rows, P(None), P(None, "tp"), P("tp", None), rows),
                         out_specs=(rows, rows, P("data", "tp"), rows, P("data")),
                         check_vma=False)
```

profile of v0, /device:TPU:1, one launch (start us, length us, event | category | flops | bytes accessed | tf_op | source)
XLA Modules:
  0.0 669.5 jit_solution(11444211686411728604)
XLA Ops:
  7.2 0.0 copy-start
  7.2 0.0 copy-start.4
  7.2 0.0 all-gather.5.cloned.1.call-start
  7.2 0.7 all-gather.5.cloned.1.call-update
  7.9 0.0 all-gather.3.cloned.1.call-start
  8.0 1.6 convert_reduce_fusion
  9.5 1.8 fusion.20
  11.4 2.8 fusion.13
  14.2 0.0 all-gather.3.cloned.1.call-update
  14.2 0.0 reduce-scatter.5.cloned.1.call-start
  14.3 96.8 %all-gather.5.cloned.1.call-done = bf16[4096,1280]{1,0:T(8,128)(2,1)} async-done(((bf16[512,1280]{1,0:T(8,128)(2,1)}), bf16[4096,1280]{1,0:T(8,128)(2,1)}) %all-gather.5.cloned.1.call-update) | async-done | bytes 10485776 | tf_op jit(solution)/shard_map/all_gather | solution.py:40
  111.0 0.0 copy-done.4
  111.0 13.5 %fusion.24 = f32[4096,640]{1,0:T(8,128)} fusion(bf16[4096,1280]{1,0:T(8,128)(2,1)} %all-gather.5.cloned.1.call-done, bf16[640,1280]{1,0:T(8,128)(2,1)S(1)} %copy-done.4), kind=kOutput, calls=%fused_computation.35 | convolution fusion | flops 6710886400 | bytes 22609920 | tf_op jit(solution)/shard_map/dot_general | solution.py:26
  124.5 86.5 %all-gather.3.cloned.1.call-done = bf16[4096,1280]{1,0:T(8,128)(2,1)} async-done(((bf16[512,1280]{1,0:T(8,128)(2,1)}), bf16[4096,1280]{1,0:T(8,128)(2,1)}) %all-gather.3.cloned.1.call-update) | async-done | bytes 10485776 | tf_op jit(solution)/shard_map/all_gather | solution.py:35
  211.0 0.0 copy-done
  211.0 20.1 %fusion.6 = (bf16[4096,640]{1,0:T(8,128)(2,1)S(1)}, f32[4096,640]{1,0:T(8,128)}) fusion(f32[4096,640]{1,0:T(8,128)} %fusion.24, bf16[4096,1280]{1,0:T(8,128)(2,1)} %all-gather.3.cloned.1.call-done, bf16[1280,640]{1,0:T(8,128)(2,1)S(1)} %copy-done), kind=kOutput, calls=%fused_computation.8 | convolution fusion | flops 6763315200 | bytes 38338560 | tf_op jit(solution)/shard_map/dot_general | solution.py:36
  231.1 0.0 copy-start.5
  231.1 2.3 copy-done.5
  233.4 11.7 %fusion.25 = f32[4096,1280]{1,0:T(8,128)} fusion(bf16[4096,640]{1,0:T(8,128)(2,1)S(1)} %get-tuple-element.10, bf16[1280,640]{1,0:T(8,128)(2,1)S(1)} %copy-done), kind=kOutput, calls=%fused_computation.36 | convolution fusion | flops 6710886400 | bytes 27852800 | tf_op jit(solution)/shard_map/dot_general | solution.py:26
  245.1 0.0 reduce-scatter.5.cloned.1.call-update
  245.1 0.0 reduce-scatter.3.cloned.1.call-start
  245.2 16.7 %fusion.23 = f32[4096,1280]{1,0:T(8,128)} fusion(bf16[640,1280]{1,0:T(8,128)(2,1)S(1)} %copy-done.4, f32[4096,640]{1,0:T(8,128)} %get-tuple-element.11), kind=kOutput, calls=%fused_computation.34 | convolution fusion | flops 6734479360 | bytes 33095680 | tf_op jit(solution)/shard_map/dot_general | solution.py:38
  261.9 0.0 reduce-scatter.3.cloned.1.call-update
  261.9 13.8 %fusion.26 = f32[1280,640]{1,0:T(8,128)} fusion(bf16[4096,1280]{1,0:T(8,128)(2,1)} %all-gather.3.cloned.1.call-done, bf16[4096,640]{1,0:T(8,128)(2,1)} %copy-done.5), kind=kOutput, calls=%fused_computation.37 | convolution fusion | flops 6710886400 | bytes 19005440 | tf_op jit(solution)/shard_map/dot_general | solution.py:22
  275.7 0.0 copy-start.2
  275.7 0.0 copy-start.3
  275.7 16.5 %fusion.22 = f32[640,1280]{1,0:T(8,128)} fusion(bf16[4096,1280]{1,0:T(8,128)(2,1)} %all-gather.5.cloned.1.call-done, f32[4096,640]{1,0:T(8,128)} %get-tuple-element.11), kind=kOutput, calls=%fused_computation.33 | convolution fusion | flops 6734479360 | bytes 24248320 | tf_op jit(solution)/shard_map/dot_general | solution.py:22
  292.2 157.1 %reduce-scatter.5.cloned.1.call-done = f32[512,1280]{1,0:T(8,128)} async-done(((f32[4096,1280]{1,0:T(8,128)}), f32[512,1280]{1,0:T(8,128)}) %reduce-scatter.5.cloned.1.call-update) | async-done | bytes 2621456 | tf_op jit(solution)/shard_map/reduce_scatter | solution.py:45
  449.3 0.0 copy-done.2
  449.3 0.0 copy-done.3
  449.3 2.8 fusion.19
  452.1 16.5 %psum.7 = f32[1280]{0:T(1024)} all-reduce(f32[1280]{0:T(1024)S(1)} %get-tuple-element.5), channel_id=1, replica_groups=mesh['data'=4,'tp'=8] {'tp'}, use_global_device_ids=true, to_apply=%region_7.0 | all-reduce | flops 1280 | bytes 10240 | tf_op jit(solution)/shard_map/psum | solution.py:46
  468.7 189.5 %reduce-scatter.3.cloned.1.call-done = f32[512,1280]{1,0:T(8,128)} async-done(((f32[4096,1280]{1,0:T(8,128)}), f32[512,1280]{1,0:T(8,128)}) %reduce-scatter.3.cloned.1.call-update) | async-done | bytes 2621456 | tf_op jit(solution)/shard_map/reduce_scatter | solution.py:39
  658.2 0.0 copy-start.1
  658.2 4.8 fusion.18
  663.0 0.0 copy-done.1
  (3 shorter events, 0.0 us)
Async XLA Ops:
  7.2 203.8 %copy-start = (bf16[1280,640]{1,0:T(8,128)(2,1)S(1)}, bf16[1280,640]{1,0:T(8,128)(2,1)}, u32[]{:S(2)}) copy-start(bf16[1280,640]{1,0:T(8,128)(2,1)} %param.7) | copy-start | bytes 4915204
  7.2 103.9 %copy-start.4 = (bf16[640,1280]{1,0:T(8,128)(2,1)S(1)}, bf16[640,1280]{1,0:T(8,128)(2,1)}, u32[]{:S(2)}) copy-start(bf16[640,1280]{1,0:T(8,128)(2,1)} %param.8) | copy-start | bytes 4915204
  7.2 103.8 %all-gather.5.cloned.1.call-start = ((), (), s32[]{:S(2)}) async-start(), calls=%async_computation.4 | async-start | bytes 11796480 | tf_op jit(solution)/shard_map/all_gather | solution.py:40
  7.9 203.0 %all-gather.3.cloned.1.call-start = ((), (), s32[]{:S(2)}) async-start(), calls=%async_computation.2 | async-start | bytes 11796480 | tf_op jit(solution)/shard_map/all_gather | solution.py:35
  14.2 435.1 %reduce-scatter.5.cloned.1.call-start = ((), (), s32[]{:S(2)}) async-start(), calls=%async_computation.5 | async-start | bytes 23592960 | tf_op jit(solution)/shard_map/reduce_scatter | solution.py:45
  231.1 2.3 copy-start.5
  245.1 413.1 %reduce-scatter.3.cloned.1.call-start = ((), (), s32[]{:S(2)}) async-start(), calls=%async_computation.3 | async-start | bytes 23592960 | tf_op jit(solution)/shard_map/reduce_scatter | solution.py:39
  275.7 173.6 %copy-start.2 = (bf16[512,1280]{1,0:T(8,128)(2,1)S(1)}, bf16[512,1280]{1,0:T(8,128)(2,1)}, u32[]{:S(2)}) copy-start(bf16[512,1280]{1,0:T(8,128)(2,1)} %param.5) | copy-start | bytes 3932164
  275.7 173.6 %copy-start.3 = (f32[1280]{0:T(1024)S(1)}, f32[1280]{0:T(1024)}, u32[]{:S(2)}) copy-start(f32[1280]{0:T(1024)} %param.6) | copy-start | bytes 15364
  658.2 4.8 copy-start.1
Sparse Core Ops, SparseCore 0:
  9.6 101.3 all-gather.4
  113.2 97.6 all-gather.2
  245.2 204.0 reduce-scatter.4
  451.5 206.6 reduce-scatter.2
where the time goes:
time: 672 us; the launch traced here: 670 us
  waiting for transfers between devices  531 us (79%)
  matrix products  92.3 us (14%)
  blocking collectives  16.5 us (2%)
  other arithmetic  13.8 us (2%)
  between operations  13.8 us (2%)
    reduce_scatter x1, waiting for transfers between devices, body(): lax.psum_scatter(Yp, 'tp', scatter_dimension=0, tiled=True)  190 us
    reduce_scatter x1, waiting for transfers between devices, body(): dXn = lax.psum_scatter(_nt(dA, W1), 'tp', scatter_dimension=0, tiled=True)  157 us
    all_gather x1, waiting for transfers between devices, body(): g = lax.all_gather(dY, 'tp', axis=0, tiled=True)  96.8 us
    all_gather x1, waiting for transfers between devices, body(): lax.all_gather((xhatv * gamma).astype(jnp.bfloat16), 'tp', axis=0, tiled=...  86.5 us
    dot_general x2, matrix products, _tn(): lax.dot_general(a, b, (((0,), (0,)), ((), ())), preferred_element_type=jn...  30.3 us
    dot_general x2, matrix products, _nt(): lax.dot_general(a, b, (((1,), (1,)), ((), ())), preferred_element_type=jn...  25.1 us
    dot_general x1, matrix products, body(): A = jnp.dot(Xn, W1, preferred_element_type=jnp.float32)  20.1 us
    dot_general x1, matrix products, body(): Yp = jnp.dot(H, W2, preferred_element_type=jnp.float32)  16.7 us
  transfers between devices with their start and end apart: 4, of which 4 were waited for; matrix products, arithmetic and copies ran while one was open for 10% of the time, Pallas kernels for 0%

commit v1 on v0

v1 whole, which is shorter than its diff:
```python
import functools

import jax
import jax.numpy as jnp
from jax import lax
from jax.experimental import pallas as pl
from jax.experimental.pallas import tpu as pltpu
from jax.sharding import PartitionSpec as P

EPS = 1e-6
D = 1280
TOK = 512
FF = 640
NH = 2
TH = TOK // NH
NB = 256
RT = 64
K0 = 0.7978845608028654
K1 = 0.044715
MESH = pl.DeviceIdType.MESH


def _nt(a, b):
    return lax.dot_general(a, b, (((1,), (1,)), ((), ())), preferred_element_type=jnp.float32)


def _nn(a, b):
    return lax.dot_general(a, b, (((1,), (0,)), ((), ())), preferred_element_type=jnp.float32)


def _ln(x):
    mu = jnp.mean(x, axis=-1, keepdims=True)
    xc = x - mu
    var = jnp.mean(xc * xc, axis=-1, keepdims=True)
    rstd = lax.rsqrt(var + EPS)
    return xc * rstd, rstd


def _gelu_pair(a, g):
    a2 = a * a
    t = jnp.tanh(a * (K0 + (K0 * K1) * a2))
    cdf = 0.5 + 0.5 * t
    h = a * cdf
    dg = cdf + h * (1.0 - t) * (K0 + (3.0 * K0 * K1) * a2)
    return h.astype(jnp.bfloat16), (dg * g).astype(jnp.bfloat16)


def _kernel(x_h, g_ref, w1_h, w2_h, dy_h, y_h, dx_h, dw1_h, dw2_h, dg_ref,
            T, W, yacc, wacc, xb, ob, dgb,
            lsem, osem, tsend, trecv, wsend, wrecv, dgs, dgr):
    d = lax.axis_index("data")
    t = lax.axis_index("tp")
    z = t // 2
    c = t - 2 * z
    o = 1 - c
    partner = (d, 2 * z + o)
    up = (d, 2 * z + 2 + c)
    down = (d, 2 * z - 2 + c)
    dxn = lax.rem(d + 2, 4)
    dyn = d + 1 - 2 * lax.rem(d, 2)
    ddg = 3 - d
    side = ((dxn, 3), (dyn, 4), (ddg, 5))

    def tslot(src, lane, h):
        return T.at[src, :, pl.ds(pl.multiple_of(lane * TOK + h * TH, TH), TH), :]

    def tcopy(src, lane, h, path, dev):
        s = tslot(src, lane, h)
        return pltpu.make_async_remote_copy(
            src_ref=s, dst_ref=s, send_sem=tsend.at[src, h, path],
            recv_sem=trecv.at[src, lane, h], device_id=dev, device_id_type=MESH)

    def wcopy(src, lane, q, path, dev):
        s = W.at[src, :, pl.ds(pl.multiple_of(lane * FF + q * (FF // 4), 32), FF // 4), :]
        return pltpu.make_async_remote_copy(
            src_ref=s, dst_ref=s, send_sem=wsend.at[src, q, path],
            recv_sem=wrecv.at[src, lane, q], device_id=dev, device_id_type=MESH)

    def wown(lane):
        s = W.at[z, :, pl.ds(pl.multiple_of(lane * FF, FF), FF), :]
        return pltpu.make_async_remote_copy(
            src_ref=s, dst_ref=s, send_sem=wsend.at[z, 0, 2],
            recv_sem=wrecv.at[z, lane, 0], device_id=partner, device_id_type=MESH)

    frow = pl.ds(pl.multiple_of(c * FF, FF), FF)
    trow = pl.ds(pl.multiple_of(c * TOK, TOK), TOK)
    l1 = pltpu.make_async_copy(w1_h, W.at[z, 0, frow, :], lsem.at[0])
    l2 = pltpu.make_async_copy(w2_h, W.at[z, 1, frow, :], lsem.at[1])
    l3 = pltpu.make_async_copy(x_h, xb, lsem.at[2])
    l4 = pltpu.make_async_copy(dy_h, T.at[z, 1, trow, :], lsem.at[3])
    l1.start(); l2.start(); l3.start(); l4.start()
    l1.wait(); l2.wait()

    @pl.when(z < 3)
    def _():
        wcopy(z, c, d, 0, up).start()

    @pl.when(z > 0)
    def _():
        wcopy(z, c, d, 1, down).start()

    wown(c).start()
    l3.wait()

    @pl.loop(0, TOK // RT)
    def _(i):
        r = pl.ds(pl.multiple_of(i * RT, RT), RT)
        x = xb[r, :].astype(jnp.float32)
        xh, _ = _ln(x)
        T[z, 0, pl.ds(pl.multiple_of(c * TOK + i * RT, RT), RT), :] = (xh * g_ref[...]).astype(jnp.bfloat16)
        yacc[1, r, :] = x
        yacc[0, r, :] = jnp.zeros((RT, D), jnp.float32)

    l4.wait()

    @pl.loop(0, FF // RT)
    def _(i):
        r = pl.ds(pl.multiple_of(i * RT, RT), RT)
        wacc[0, r, :] = jnp.zeros((RT, D), jnp.float32)
        wacc[1, r, :] = jnp.zeros((RT, D), jnp.float32)

    def tup():
        for h in range(NH):
            tcopy(z, c, h, 0, up).start()

    def tdown():
        for h in range(NH):
            tcopy(z, c, h, 1, down).start()

    pl.when(z == 0)(tup)
    pl.when(z == 3)(tdown)
    for h in range(NH):
        tcopy(z, c, h, 2, partner).start()

    for s in range(1, 4):
        for sgn in (-1, 1):
            src = z + sgn * s

            @pl.when((src >= 0) & (src <= 3))
            def _():
                wcopy(src, c, d, 0, up).wait_recv()

                @pl.when((z + (-sgn) >= 0) & (z + (-sgn) <= 3))
                def _():
                    wcopy(src, c, d, 0, (d, 2 * (z - sgn) + c)).start()

                for dd, path in side:
                    wcopy(src, c, d, path, (dd, t)).start()
                wcopy(src, c, d, 2, partner).start()

        if s < 3:
            pl.when(z == s)(tup)
            pl.when(z == 3 - s)(tdown)

    def block(L, li, lrow, m, R, ri, r0, nb, acc):
        rr = pl.ds(pl.multiple_of(r0, 128), nb)
        lr = pl.ds(pl.multiple_of(lrow, 128), m)
        a = _nt(L[li, 0, lr, :], R[ri, 0, rr, :])
        g = _nt(L[li, 1, lr, :], R[ri, 1, rr, :])
        h, da = _gelu_pair(a, g)
        acc[1, :, :] += _nn(h, R[ri, 1, rr, :])
        acc[0, :, :] += _nn(da, R[ri, 0, rr, :])

    elast = jnp.where(z == 0, 6, jnp.where(z == 3, 5, jnp.where(z == 1, 4, 3)))

    @pl.loop(0, 7)
    def _(e):
        s = (e + 1) // 2
        sgn = 1 - 2 * (e - 2 * (e // 2))
        src = z + sgn * s
        nxt = z - sgn

        @pl.when((src >= 0) & (src <= 3))
        def _():
            @pl.when(e == 0)
            def _():
                wown(o).wait_recv()

            @pl.when(e > 0)
            def _():
                for dd, _p in side:
                    wcopy(src, c, dd, 2, partner).wait_recv()
                    wcopy(src, c, dd, 2, partner).start()
                for q in range(4):
                    wcopy(src, o, q, 2, partner).wait_recv()

            @pl.loop(0, 2 * FF // NB)
            def _(i):
                block(T, z, c * TOK, TOK, W, src, i * NB, NB, yacc)

            @pl.when(e == elast)
            def _():
                dgb[t] = jnp.zeros((8, D), jnp.float32)

                @pl.loop(0, TOK // RT)
                def _(i):
                    r = pl.ds(pl.multiple_of(i * RT, RT), RT)
                    x = xb[r, :].astype(jnp.float32)
                    xh, rstd = _ln(x)
                    dxn_ = yacc[0, r, :]
                    p = dxn_ * xh
                    dgb[t] += jnp.sum(p.reshape(RT // 8, 8, D), axis=0)
                    dxh = dxn_ * g_ref[...]
                    m1 = jnp.mean(dxh, axis=-1, keepdims=True)
                    m2 = jnp.mean(dxh * xh, axis=-1, keepdims=True)
                    dyv = T[z, 1, pl.ds(pl.multiple_of(c * TOK + i * RT, RT), RT), :].astype(jnp.float32)
                    ob[r, :] = (dyv + rstd * (dxh - m1 - xh * m2)).astype(jnp.bfloat16)
                    xb[r, :] = yacc[1, r, :].astype(jnp.bfloat16)

                pltpu.make_async_copy(xb, y_h, osem.at[0]).start()
                pltpu.make_async_copy(ob, dx_h, osem.at[1]).start()
                for k in range(1, 8):
                    pltpu.make_async_remote_copy(
                        src_ref=dgb.at[t], dst_ref=dgb.at[t], send_sem=dgs.at[k],
                        recv_sem=dgr.at[k], device_id=(d, lax.rem(t + k, 8)),
                        device_id_type=MESH).start()

            for h in range(NH):
                @pl.when(e > 0)
                def _():
                    tcopy(src, c, h, 0, up).wait_recv()

                    @pl.when((nxt >= 0) & (nxt <= 3))
                    def _():
                        tcopy(src, c, h, 0, (d, 2 * nxt + c)).start()

                    tcopy(src, c, h, 2, partner).start()

            @pl.loop(0, NH)
            def _(h):
                @pl.loop(0, 2)
                def _(j):
                    lane = c + j * (1 - 2 * c)

                    @pl.when(j == 1)
                    def _():
                        tcopy(src, o, h, 2, partner).wait_recv()

                    block(W, z, c * FF, FF, T, src, lane * TOK + h * TH, TH, wacc)

    ow1 = pltpu.make_async_copy(wacc.at[0], dw1_h, osem.at[2])
    ow2 = pltpu.make_async_copy(wacc.at[1], dw2_h, osem.at[3])
    ow1.start()
    ow2.start()

    for k in range(1, 8):
        pltpu.make_async_remote_copy(
            src_ref=dgb.at[t], dst_ref=dgb.at[t], send_sem=dgs.at[k],
            recv_sem=dgr.at[k], device_id=partner, device_id_type=MESH).wait_recv()
    tot = jnp.sum(dgb[...], axis=0)
    dg_ref[...] = jnp.sum(tot, axis=0, keepdims=True)

    for k in range(1, 8):
        pltpu.make_async_remote_copy(
            src_ref=dgb.at[t], dst_ref=dgb.at[t], send_sem=dgs.at[k],
            recv_sem=dgr.at[k], device_id=partner, device_id_type=MESH).wait_send()
    wown(c).wait_send()

    @pl.when(z < 3)
    def _():
        wcopy(z, c, d, 0, up).wait_send()
        for h in range(NH):
            tcopy(z, c, h, 0, up).wait_send()

    @pl.when(z > 0)
    def _():
        wcopy(z, c, d, 1, down).wait_send()
        for h in range(NH):
            tcopy(z, c, h, 1, down).wait_send()

    for h in range(NH):
        tcopy(z, c, h, 2, partner).wait_send()

    @pl.loop(1, 7)
    def _(e):
        s = (e + 1) // 2
        sgn = 1 - 2 * (e - 2 * (e // 2))
        src = z + sgn * s
        nxt = z - sgn

        @pl.when((src >= 0) & (src <= 3))
        def _():
            @pl.when((nxt >= 0) & (nxt <= 3))
            def _():
                wcopy(src, c, d, 0, up).wait_send()
                for h in range(NH):
                    tcopy(src, c, h, 0, up).wait_send()

            for dd, path in side:
                wcopy(src, c, d, path, partner).wait_send()
                wcopy(src, c, dd, 2, partner).wait_send()
            wcopy(src, c, d, 2, partner).wait_send()
            for h in range(NH):
                tcopy(src, c, h, 2, partner).wait_send()

    pltpu.make_async_copy(xb, y_h, osem.at[0]).wait()
    pltpu.make_async_copy(ob, dx_h, osem.at[1]).wait()
    ow1.wait()
    ow2.wait()


def solution(mesh):
    rows = P(("data", "tp"), None)
    bf, f32 = jnp.bfloat16, jnp.float32

    def body(X, gamma, W1, W2, dY):
        hbm = pl.BlockSpec(memory_space=pl.ANY)
        vm = pl.BlockSpec(memory_space=pltpu.VMEM)
        Y, dX, dW1t, dW2, dg = pl.pallas_call(
            _kernel,
            name="mlp_block",
            out_shape=(jax.ShapeDtypeStruct((TOK, D), bf), jax.ShapeDtypeStruct((TOK, D), bf),
                       jax.ShapeDtypeStruct((FF, D), f32), jax.ShapeDtypeStruct((FF, D), f32),
                       jax.ShapeDtypeStruct((1, D), f32)),
            in_specs=[hbm, vm, hbm, hbm, hbm],
            out_specs=[hbm, hbm, hbm, hbm, vm],
            scratch_shapes=[
                pltpu.VMEM((4, 2, 2 * TOK, D), bf),
                pltpu.VMEM((4, 2, 2 * FF, D), bf),
                pltpu.VMEM((2, TOK, D), f32),
                pltpu.VMEM((2, FF, D), f32),
                pltpu.VMEM((TOK, D), bf),
                pltpu.VMEM((TOK, D), bf),
                pltpu.VMEM((8, 8, D), f32),
                pltpu.SemaphoreType.DMA((4,)),
                pltpu.SemaphoreType.DMA((4,)),
                pltpu.SemaphoreType.DMA((4, NH, 3)),
                pltpu.SemaphoreType.DMA((4, 2, NH)),
                pltpu.SemaphoreType.DMA((4, 4, 6)),
                pltpu.SemaphoreType.DMA((4, 2, 4)),
                pltpu.SemaphoreType.DMA((8,)),
                pltpu.SemaphoreType.DMA((8,)),
            ],
            compiler_params=pltpu.CompilerParams(has_side_effects=True, vmem_limit_bytes=67043328),
        )(X, gamma.reshape(1, D), W1.T, W2, dY)
        return Y, dX, dW1t.T, dW2, dg.reshape(D)

    return jax.shard_map(body, mesh=mesh,
                         in_specs=(rows, P(None), P(None, "tp"), P("tp", None), rows),
                         out_specs=(rows, rows, P("data", "tp"), rows, P("data")),
                         check_vma=False)
```

time: 672 us -> 270 us (0.40)
  waiting for transfers between devices: 531 us -> 0 us
  Pallas kernels: 0 us -> 251 us
  matrix products: 92.3 us -> 0 us
  blocking collectives: 16.5 us -> 0 us
  other arithmetic: 13.8 us -> 0.62 us
  between operations: 13.8 us -> 0.67 us
  local copies, waits for them, and re-layouts: 2.34 us -> 13.5 us
    reduce_scatter x2 -> x0, waiting for transfers between devices: 347 us -> none  [the longest x1 190 us: body(): lax.psum_scatter(Yp, 'tp', scatter_dimension=0, tiled=True)]
    pallas_call x0 -> x1, Pallas kernels: none -> 251 us  [body(): pl.pallas_call(_kernel, name='mlp_block', out_shape=(jax.ShapeDtypeStruct...]
    all_gather x2 -> x0, waiting for transfers between devices: 183 us -> none  [the longest x1 96.8 us: body(): g = lax.all_gather(dY, 'tp', axis=0, tiled=True)]
    dot_general x6 -> x0, matrix products: 92.3 us -> none  [the longest x2 30.3 us: _tn(): lax.dot_general(a, b, (((0,), (0,)), ((), ())), preferred_element_type=jn...]
    psum x1 -> x0, blocking collectives: 16.5 us -> none  [body(): dgamma = lax.psum(jnp.sum(dXn * xhatv, axis=0), 'tp')]
    unnamed x12 -> x15, local copies, waits for them, and re-layouts: 2.34 us -> 12.9 us
    convert_element_type x2 -> x0, other arithmetic: 7.59 us -> none  [the longest x1 4.75 us: body(): dX = (dY.astype(jnp.float32) + dx).astype(jnp.bfloat16)]
  transfers between devices with their start and end apart: 4 -> 0, of which waited for: 4 -> 0; matrix products, arithmetic and copies ran while one was open for 10% -> 0% of each run, Pallas kernels for 0% -> 0%
where the time goes in v1:
time: 270 us; the launch traced here: 266 us
  Pallas kernels  251 us (93%)
  local copies, waits for them, and re-layouts  13.5 us (5%)
    pallas_call x1, Pallas kernels, body(): pl.pallas_call(_kernel, name='mlp_block', out_shape=(jax.ShapeDtypeStruct...  251 us
    unnamed x15, local copies, waits for them, and re-layouts  12.9 us

profile of v1, /device:TPU:1, one launch (start us, length us, event | category | flops | bytes accessed | tf_op | source)
XLA Modules:
  0.0 266.2 jit_solution(8314145688860332783)
XLA Ops:
  0.6 0.0 copy-start.3
  0.6 3.5 %copy.10 = bf16[1280,640]{0,1:T(8,128)(2,1)} copy(bf16[1280,640]{1,0:T(8,128)(2,1)} %param.7) | data formatting | bytes 3276800 | tf_op args[2]
  4.2 0.0 copy-done.3
  4.2 0.6 reshape.16.g_ref
  4.8 251.4 %mlp_block.1 = (bf16[512,1280]{1,0:T(8,128)(2,1)}, bf16[512,1280]{1,0:T(8,128)(2,1)}, f32[640,1280]{1,0:T(8,128)}, f32[640,1280]{1,0:T(8,128)}, f32[1,1280]{1,0:T(1,128)}) custom-call(bf16[512,1280]{1,0:T(8,128)(2,1)} %x_h.1, f32[1,1280]{1,0:T(1,128)} %reshape.16.g_ref, bf16[640,1280]{1,0:T(8,128)(2,1)} %bitcast.2, bf16[640,1280]{1,0:T(8,128)(2,1)} %w2_h.1, ...), custom_call_target="tpu_custom_call" | custom-call | tf_op jit(solution)/shard_map/mlp_block/pallas_call | solution.py:309
  256.2 0.0 copy-start.4
  256.2 0.0 copy-start.2
  256.2 4.7 %copy.11 = f32[1280,640]{1,0:T(8,128)} copy(f32[1280,640]{0,1:T(8,128)} %bitcast.3) | data formatting | bytes 6553600
  260.9 0.0 copy-start.1
  260.9 0.0 copy-done.4
  260.9 0.6 reduce
  261.5 0.0 copy-done.2
  261.5 0.0 copy-start
  261.5 1.1 copy.15
  262.6 0.0 copy-done.1
  262.6 1.1 copy.16
  263.6 0.9 copy-done
  264.5 1.7 copy.17
Async XLA Ops:
  0.6 3.6 %copy-start.3 = (f32[1280]{0:T(1024)S(1)}, f32[1280]{0:T(1024)}, u32[]{:S(2)}) copy-start(f32[1280]{0:T(1024)} %param.6) | copy-start | bytes 15364
  256.2 4.7 %copy-start.4 = (f32[1,1280]{1,0:T(1,128)S(1)}, f32[1,1280]{1,0:T(1,128)}, u32[]{:S(2)}) copy-start(f32[1,1280]{1,0:T(1,128)} %get-tuple-element.14) | copy-start | bytes 15364
  256.2 5.3 %copy-start.2 = (bf16[512,1280]{1,0:T(8,128)(2,1)S(1)}, bf16[512,1280]{1,0:T(8,128)(2,1)}, u32[]{:S(2)}) copy-start(bf16[512,1280]{1,0:T(8,128)(2,1)} %get-tuple-element.25) | copy-start | bytes 3932164
  260.9 1.7 copy-start.1
  261.5 3.0 %copy-start = (f32[640,1280]{1,0:T(8,128)S(1)}, f32[640,1280]{1,0:T(8,128)}, u32[]{:S(2)}) copy-start(f32[640,1280]{1,0:T(8,128)} %get-tuple-element.28) | copy-start | bytes 9830404

commit v2 on v1

v2 whole, which is shorter than its diff:
```python
import functools

import jax
import jax.numpy as jnp
from jax import lax
from jax.experimental import pallas as pl
from jax.experimental.pallas import tpu as pltpu
from jax.sharding import PartitionSpec as P

EPS = 1e-6
D = 1280
TOK = 512
FF = 640
NH = 4
TH = TOK // NH
NB = 256
RT = 64
VM1 = 60 * 2**20
VM2 = 60 * 2**20
K0 = 0.7978845608028654
K1 = 0.044715
MESH = pl.DeviceIdType.MESH


def _nt(a, b):
    return lax.dot_general(a, b, (((1,), (1,)), ((), ())), preferred_element_type=jnp.float32)


def _nn(a, b):
    return lax.dot_general(a, b, (((1,), (0,)), ((), ())), preferred_element_type=jnp.float32)


def _tn(a, b):
    return lax.dot_general(a, b, (((0,), (0,)), ((), ())), preferred_element_type=jnp.float32)


def _ln(x):
    mu = jnp.mean(x, axis=-1, keepdims=True)
    xc = x - mu
    var = jnp.mean(xc * xc, axis=-1, keepdims=True)
    rstd = lax.rsqrt(var + EPS)
    return xc * rstd, rstd


def _gelu_pair(a, g):
    a2 = a * a
    t = jnp.tanh(a * (K0 + (K0 * K1) * a2))
    cdf = 0.5 + 0.5 * t
    h = a * cdf
    dg = cdf + h * (1.0 - t) * (K0 + (3.0 * K0 * K1) * a2)
    return h.astype(jnp.bfloat16), (dg * g).astype(jnp.bfloat16)


def _kernel(x_h, g_ref, w1_h, w2_h, dy_h, y_h, dx_h, dw1_h, dw2_h, tl_h, W, dg_ref,
            T, wo, wb, yacc, wacc, wt, xb, ob, dgb,
            w1n, lsem, osem, bsem, tsend, trecv, wsend, wrecv, dgs, dgr):
    d = lax.axis_index("data")
    t = lax.axis_index("tp")
    z = t // 2
    c = t - 2 * z
    o = 1 - c
    partner = (d, 2 * z + o)
    up = (d, 2 * z + 2 + c)
    down = (d, 2 * z - 2 + c)
    dxn = lax.rem(d + 2, 4)
    dyn = d + 1 - 2 * lax.rem(d, 2)
    ddg = 3 - d
    side = ((dxn, 3), (dyn, 4), (ddg, 5))

    def tslot(src, lane, h):
        return T.at[src, :, h, lane]

    def tcopy(src, lane, h, path, dev):
        s = tslot(src, lane, h)
        return pltpu.make_async_remote_copy(
            src_ref=s, dst_ref=s, send_sem=tsend.at[src, h, path],
            recv_sem=trecv.at[src, lane, h], device_id=dev, device_id_type=MESH)

    def wcopy(src, lane, q, path, dev):
        s = W.at[src, :, pl.ds(pl.multiple_of(lane * FF + q * (FF // 4), 32), FF // 4), :]
        return pltpu.make_async_remote_copy(
            src_ref=s, dst_ref=s, send_sem=wsend.at[src, q, path],
            recv_sem=wrecv.at[src, lane, q], device_id=dev, device_id_type=MESH)

    def wown(lane):
        return pltpu.make_async_remote_copy(
            src_ref=wo, dst_ref=W.at[z, :, pl.ds(pl.multiple_of(lane * FF, FF), FF), :], send_sem=wsend.at[z, 0, 2],
            recv_sem=wrecv.at[z, lane, 0], device_id=partner, device_id_type=MESH)

    frow = pl.ds(pl.multiple_of(c * FF, FF), FF)
    l1 = pltpu.make_async_copy(w1_h, w1n, lsem.at[0])
    l2 = pltpu.make_async_copy(w2_h, wo.at[1], lsem.at[1])
    l3 = pltpu.make_async_copy(x_h, xb, lsem.at[2])
    l1.start()
    l2.start()
    l3.start()
    l4 = [pltpu.make_async_copy(dy_h.at[pl.ds(h * TH, TH), :], T.at[z, 1, h, c], lsem.at[3 + h])
          for h in range(NH)]
    for cp in l4:
        cp.start()
    barrier = pltpu.get_barrier_semaphore()
    for k in range(1, 8):
        pl.semaphore_signal(barrier, inc=1, device_id=(d, lax.rem(t + k, 8)), device_id_type=MESH)
    for dd, _p in side:
        pl.semaphore_signal(barrier, inc=1, device_id=(dd, t), device_id_type=MESH)
    pl.semaphore_wait(barrier, 10)

    def whalf(mat, path, dev):
        q = pl.ds(pl.multiple_of(d * (FF // 4), 32), FF // 4)
        return pltpu.make_async_remote_copy(
            src_ref=w2_h.at[q, :] if mat else wo.at[0, q, :],
            dst_ref=W.at[z, mat, pl.ds(pl.multiple_of(c * FF + d * (FF // 4), 32), FF // 4), :], send_sem=wsend.at[z, d, path],
            recv_sem=wrecv.at[z, c, d], device_id=dev, device_id_type=MESH)

    @pl.when(z < 3)
    def _():
        whalf(1, 0, up).start()

    @pl.when(z > 0)
    def _():
        whalf(1, 1, down).start()

    l1.wait()

    for i in range(FF // 128):
        wo[0, i * 128:(i + 1) * 128, :] = w1n[:, i * 128:(i + 1) * 128].T

    l2.wait()
    l3.wait()

    @pl.loop(0, TOK // RT)
    def _(i):
        r = pl.ds(pl.multiple_of(i * RT, RT), RT)
        x = xb[r, :].astype(jnp.float32)
        xh, _ = _ln(x)
        h = i // (TH // RT)
        rr = pl.ds(pl.multiple_of((i - h * (TH // RT)) * RT, RT), RT)
        T[z, 0, h, c, rr, :] = (xh * g_ref[...].reshape(1, D)).astype(jnp.bfloat16)
        yacc[1, r, :] = x
        yacc[0, r, :] = jnp.zeros((RT, D), jnp.float32)

    @pl.when(z < 3)
    def _():
        whalf(0, 0, up).start()

    @pl.when(z > 0)
    def _():
        whalf(0, 1, down).start()

    wown(c).start()
    lo = pltpu.make_async_copy(wo, W.at[z, :, frow, :], lsem.at[3 + NH])
    lo.start()

    @pl.loop(0, FF // RT)
    def _(i):
        r = pl.ds(pl.multiple_of(i * RT, RT), RT)
        wacc[0, r, :] = jnp.zeros((RT, D), jnp.float32)
        wacc[1, r, :] = jnp.zeros((RT, D), jnp.float32)

    for cp in l4:
        cp.wait()

    def town(h0, h1):
        @pl.when(z < 3)
        def _():
            for h in range(h0, h1):
                tcopy(z, c, h, 0, up).start()

        @pl.when(z > 0)
        def _():
            for h in range(h0, h1):
                tcopy(z, c, h, 1, down).start()

    town(0, NH // 2)
    for h in range(NH):
        tcopy(z, c, h, 2, partner).start()

    def wstep(s):
        for sgn in (-1, 1):
            src = z + sgn * s

            @pl.when((src >= 0) & (src <= 3))
            def _():
                with jax.named_scope("wzwait"):
                    wcopy(src, c, d, 0, up).wait_recv()

                @pl.when((z - sgn >= 0) & (z - sgn <= 3))
                def _():
                    wcopy(src, c, d, 0, (d, 2 * (z - sgn) + c)).start()

                for dd, path in side:
                    wcopy(src, c, d, path, (dd, t)).start()
                wcopy(src, c, d, 2, partner).start()

    def block(l1, l2, r1, r2, acc):
        a = _nt(l1, r1)
        g = _nt(l2, r2)
        h, da = _gelu_pair(a, g)
        acc[1, :, :] += _nn(h, r2)
        acc[0, :, :] += _nn(da, r1)

    elast = jnp.where(z == 0, 6, jnp.where(z == 3, 5, jnp.where(z == 1, 4, 3)))

    @pl.loop(0, 7)
    def _(e):
        s = (e + 1) // 2
        sgn = 1 - 2 * (e - 2 * (e // 2))
        src = z + sgn * s
        nxt = z - sgn

        @pl.when((e == 0) | (e == 1) | (e == 3))
        def _():
            wstep(jnp.where(e == 0, 1, jnp.where(e == 1, 2, 3)))

        @pl.when(e == 0)
        def _():
            town(NH // 2, NH)

        def epilogue():
            dgb[t] = jnp.zeros((8, D), jnp.float32)

            @pl.loop(0, TOK // RT)
            def _(i):
                r = pl.ds(pl.multiple_of(i * RT, RT), RT)
                x = xb[r, :].astype(jnp.float32)
                xh, rstd = _ln(x)
                dxn_ = yacc[0, r, :]
                p = dxn_ * xh
                dgb[t] += jnp.sum(p.reshape(RT // 8, 8, D), axis=0)
                dxh = dxn_ * g_ref[...].reshape(1, D)
                m1 = jnp.mean(dxh, axis=-1, keepdims=True)
                m2 = jnp.mean(dxh * xh, axis=-1, keepdims=True)
                h = i // (TH // RT)
                rr = pl.ds(pl.multiple_of((i - h * (TH // RT)) * RT, RT), RT)
                dyv = T[z, 1, h, c, rr, :].astype(jnp.float32)
                ob[r, :] = (dyv + rstd * (dxh - m1 - xh * m2)).astype(jnp.bfloat16)
                xb[r, :] = yacc[1, r, :].astype(jnp.bfloat16)

            pltpu.make_async_copy(xb, y_h, osem.at[0]).start()
            pltpu.make_async_copy(ob, dx_h, osem.at[1]).start()
            for k in range(1, 8):
                pltpu.make_async_remote_copy(
                    src_ref=dgb.at[t], dst_ref=dgb.at[t], send_sem=dgs.at[k],
                    recv_sem=dgr.at[k], device_id=(d, lax.rem(t + k, 8)),
                    device_id_type=MESH).start()

        def flush():
            with jax.named_scope("flush"):
                pltpu.make_async_copy(wacc.at[1], dw2_h, osem.at[3]).start()
                for i in range(FF // 128):
                    wt[:, i * 128:(i + 1) * 128] = wacc[0, i * 128:(i + 1) * 128, :].T
                pltpu.make_async_copy(wt, dw1_h, osem.at[2]).start()

        def wpart():
            @pl.when(e == 0)
            def _():
                wown(o).wait_recv()
                lo.wait()

            @pl.when(e > 0)
            def _():
                with jax.named_scope("wxywait"):
                    for dd, _p in side:
                        wcopy(src, c, dd, 2, partner).wait_recv()
                        wcopy(src, c, dd, 2, partner).start()
                with jax.named_scope("wd2dwait"):
                    for q in range(4):
                        wcopy(src, o, q, 2, partner).wait_recv()

            with jax.named_scope("tokside"):
                def fetch(i):
                    j = lax.rem(i, 2)
                    rr = pl.ds(pl.multiple_of(i * NB, NB), NB)
                    return pltpu.make_async_copy(W.at[src, :, rr, :], wb.at[j], bsem.at[j])

                fetch(0).start()

                @pl.loop(0, 2 * FF // NB)
                def _(i):
                    @pl.when(i + 1 < 2 * FF // NB)
                    def _():
                        fetch(i + 1).start()

                    fetch(i).wait()
                    j = lax.rem(i, 2)
                    block(T[z, 0, :, c].reshape(TOK, D), T[z, 1, :, c].reshape(TOK, D),
                          wb[j, 0], wb[j, 1], yacc)

            pl.when(e == elast)(epilogue)

        @pl.when((src >= 0) & (src <= 3))
        def _():
            @pl.loop(0, NH)
            def _(h):
                pl.when(h == NH // 2)(wpart)
                last = (e == elast) & (h == NH - 1)
                pl.when(last)(flush)

                @pl.when(e > 0)
                def _():
                    with jax.named_scope("tzwait"):
                        tcopy(src, c, h, 0, up).wait_recv()

                    @pl.when((nxt >= 0) & (nxt <= 3))
                    def _():
                        tcopy(src, c, h, 0, (d, 2 * nxt + c)).start()

                    tcopy(src, c, h, 2, partner).start()

                with jax.named_scope("td2dwait"):
                    tcopy(src, o, h, 2, partner).wait_recv()

                @pl.when(last)
                def _():
                    with jax.named_scope("tlast"):
                        cp = pltpu.make_async_copy(T.at[src, :, NH - 1], tl_h, osem.at[4])
                        cp.start()
                        cp.wait()

                @pl.when(jnp.logical_not(last))
                def _():
                    with jax.named_scope("fside"):
                        block(wo[0], wo[1], T[src, 0, h].reshape(2 * TH, D),
                              T[src, 1, h].reshape(2 * TH, D), wacc)

    for k in range(1, 8):
        pltpu.make_async_remote_copy(
            src_ref=dgb.at[t], dst_ref=dgb.at[t], send_sem=dgs.at[k],
            recv_sem=dgr.at[k], device_id=partner, device_id_type=MESH).wait_recv()
    dg_ref[...] = jnp.sum(jnp.sum(dgb[...], axis=0), axis=0)

    for k in range(1, 8):
        pltpu.make_async_remote_copy(
            src_ref=dgb.at[t], dst_ref=dgb.at[t], send_sem=dgs.at[k],
            recv_sem=dgr.at[k], device_id=partner, device_id_type=MESH).wait_send()
    wown(c).wait_send()

    @pl.when(z < 3)
    def _():
        wcopy(z, c, d, 0, up).wait_send()
        for h in range(NH):
            tcopy(z, c, h, 0, up).wait_send()

    @pl.when(z > 0)
    def _():
        wcopy(z, c, d, 1, down).wait_send()
        for h in range(NH):
            tcopy(z, c, h, 1, down).wait_send()

    for h in range(NH):
        tcopy(z, c, h, 2, partner).wait_send()

    @pl.loop(1, 7)
    def _(e):
        s = (e + 1) // 2
        sgn = 1 - 2 * (e - 2 * (e // 2))
        src = z + sgn * s
        nxt = z - sgn

        @pl.when((src >= 0) & (src <= 3))
        def _():
            @pl.when((nxt >= 0) & (nxt <= 3))
            def _():
                wcopy(src, c, d, 0, up).wait_send()
                for h in range(NH):
                    tcopy(src, c, h, 0, up).wait_send()

            for dd, path in side:
                wcopy(src, c, d, path, partner).wait_send()
                wcopy(src, c, dd, 2, partner).wait_send()
            wcopy(src, c, d, 2, partner).wait_send()
            for h in range(NH):
                tcopy(src, c, h, 2, partner).wait_send()

    pltpu.make_async_copy(xb, y_h, osem.at[0]).wait()
    pltpu.make_async_copy(ob, dx_h, osem.at[1]).wait()
    with jax.named_scope("owait"):
        pltpu.make_async_copy(wt, dw1_h, osem.at[2]).wait()
        pltpu.make_async_copy(wacc.at[1], dw2_h, osem.at[3]).wait()


def _finish(tl_h, w1_h, w2_h, p1_h, p2_h, yp_h, dxp_h, dgp_h, y_h, dx_h, dw1_h, dw2_h, dg_h,
            tl, w1, w2, a1, a2, yv, dxv, dgv, isem, osem):
    ins = [pltpu.make_async_copy(src, dst, isem.at[i]) for i, (src, dst) in enumerate(
        ((tl_h, tl), (w1_h, w1), (w2_h, w2), (p2_h, a2), (p1_h, a1), (yp_h, yv), (dxp_h, dxv), (dgp_h, dgv)))]
    for cp in ins:
        cp.start()
    ins[0].wait()
    xn = tl[0].reshape(2 * TH, D)
    dy = tl[1].reshape(2 * TH, D)
    ins[1].wait()
    a = _nn(xn, w1[...])
    ins[2].wait()
    g = _nt(dy, w2[...])
    h, da = _gelu_pair(a, g)
    outs = []

    def out(src, dst):
        cp = pltpu.make_async_copy(src, dst, osem.at[len(outs)])
        cp.start()
        outs.append(cp)

    for i, (src, dst) in ((5, (yv, y_h)), (6, (dxv, dx_h)), (7, (dgv, dg_h))):
        ins[i].wait()
        out(src, dst)
    ins[3].wait()
    for k in range(FF // 128):
        r = slice(k * 128, (k + 1) * 128)
        a2[r, :] += _tn(h[:, r], dy)
        out(a2.at[r, :], dw2_h.at[r, :])
    ins[4].wait()
    for k in range(D // 256):
        r = slice(k * 256, (k + 1) * 256)
        a1[r, :] += _tn(xn[:, r], da)
        out(a1.at[r, :], dw1_h.at[r, :])
    for cp in outs:
        cp.wait()


def solution(mesh):
    rows = P(("data", "tp"), None)
    bf, f32 = jnp.bfloat16, jnp.float32

    def body(X, gamma, W1, W2, dY):
        hbm = pl.BlockSpec(memory_space=pl.ANY)
        vm = pl.BlockSpec(memory_space=pltpu.VMEM)
        sd = jax.ShapeDtypeStruct
        dma = pltpu.SemaphoreType.DMA
        Yp, dXp, p1, p2, tl, _, dgp = pl.pallas_call(
            _kernel,
            name="mlp_gather",
            out_shape=(sd((TOK, D), bf), sd((TOK, D), bf), sd((D, FF), f32), sd((FF, D), f32),
                       sd((2, 2, TH, D), bf), sd((4, 2, 2 * FF, D), bf), sd((D,), f32)),
            in_specs=[hbm, vm, hbm, hbm, hbm],
            out_specs=[hbm] * 6 + [vm],
            scratch_shapes=[
                pltpu.VMEM((4, 2, NH, 2, TH, D), bf),
                pltpu.VMEM((2, FF, D), bf),
                pltpu.VMEM((2, 2, NB, D), bf),
                pltpu.VMEM((2, TOK, D), f32),
                pltpu.VMEM((2, FF, D), f32),
                pltpu.VMEM((D, FF), f32),
                pltpu.VMEM((TOK, D), bf),
                pltpu.VMEM((TOK, D), bf),
                pltpu.VMEM((8, 8, D), f32),
                pltpu.VMEM((D, FF), bf),
                dma((4 + NH,)),
                dma((5,)),
                dma((2,)),
                dma((4, NH, 3)),
                dma((4, 2, NH)),
                dma((4, 4, 6)),
                dma((4, 2, 4)),
                dma((8,)),
                dma((8,)),
            ],
            compiler_params=pltpu.CompilerParams(collective_id=0, has_side_effects=True, vmem_limit_bytes=VM1),
        )(X, gamma, W1, W2, dY)
        return pl.pallas_call(
            _finish,
            name="mlp_finish",
            out_shape=(sd((TOK, D), bf), sd((TOK, D), bf), sd((D, FF), f32), sd((FF, D), f32), sd((D,), f32)),
            in_specs=[hbm] * 8,
            out_specs=[hbm] * 5,
            scratch_shapes=[
                pltpu.VMEM((2, 2, TH, D), bf),
                pltpu.VMEM((D, FF), bf),
                pltpu.VMEM((FF, D), bf),
                pltpu.VMEM((D, FF), f32),
                pltpu.VMEM((FF, D), f32),
                pltpu.VMEM((TOK, D), bf),
                pltpu.VMEM((TOK, D), bf),
                pltpu.VMEM((D,), f32),
                dma((8,)),
                dma((13,)),
            ],
            compiler_params=pltpu.CompilerParams(vmem_limit_bytes=VM2),
        )(tl, W1, W2, p1, p2, Yp, dXp, dgp)

    return jax.shard_map(body, mesh=mesh,
                         in_specs=(rows, P(None), P(None, "tp"), P("tp", None), rows),
                         out_specs=(rows, rows, P("data", "tp"), rows, P("data")),
                         check_vma=False)
```

time: 270 us -> 249 us (0.922); the launches traced: 266 us -> 249 us
  local copies, waits for them, and re-layouts: 13.5 us -> 0 us
  Pallas kernels: 251 us -> 248 us
    unnamed x15 -> x0, local copies, waits for them, and re-layouts: 12.9 us -> none
    pallas_call x1 -> x2, Pallas kernels: 251 us -> 248 us  [the longest x1 240 us: body(): pl.pallas_call(_kernel, name='mlp_gather', out_shape=(sd((TOK, D), bf), s...]
where the time goes in v2:
time: 249 us
  Pallas kernels  248 us (100%)
    pallas_call x1, Pallas kernels, body(): pl.pallas_call(_kernel, name='mlp_gather', out_shape=(sd((TOK, D), bf), s...  240 us
    pallas_call x1, Pallas kernels, body(): pl.pallas_call(_finish, name='mlp_finish', out_shape=(sd((TOK, D), bf), s...  8.28 us

profile of v2, /device:TPU:1, one launch (start us, length us, event | category | flops | bytes accessed | tf_op | source)
XLA Modules:
  0.0 248.9 jit_solution(15996424977970323941)
XLA Ops:
  0.6 240.0 %mlp_gather.1 = (bf16[512,1280]{1,0:T(8,128)(2,1)}, bf16[512,1280]{1,0:T(8,128)(2,1)}, f32[1280,640]{1,0:T(8,128)}, f32[640,1280]{1,0:T(8,128)}, bf16[2,2,128,12...) custom-call(bf16[512,1280]{1,0:T(8,128)(2,1)} %x_h.1, f32[1280]{0:T(1024)} %g_ref.1, ...), custom_call_target="tpu_custom_call" | custom-call | tf_op jit(solution)/shard_map/mlp_gather/pallas_call | solution.py:429
  240.6 8.3 %mlp_finish.1 = (bf16[512,1280]{1,0:T(8,128)(2,1)}, bf16[512,1280]{1,0:T(8,128)(2,1)}, f32[1280,640]{1,0:T(8,128)}, f32[640,1280]{1,0:T(8,128)}, f32[1280]{0:T(1024)}) custom-call(bf16[2,2,128,1280]{3,2,1,0:T(8,128)(2,1)} %get-tuple-element.11.tl_h, bf16[1280,640]{1,0:T(8,128)(2,1)} %w1_h.3, bf16[640,1280]{1,0:T(8,128)(2,1)} %w2_h.3, ...), custom_call_target="tpu_custom_call" | custom-call | tf_op jit(solution)/shard_map/mlp_finish/pallas_call | solution.py:459

commit v3 on v2

--- a/solution.py
+++ b/solution.py
@@ -15,6 +15,7 @@
 TH = TOK // NH
 NB = 256
 RT = 64
+STRIPS = ((0, 384), (384, 640))
 VM1 = 60 * 2**20
 VM2 = 60 * 2**20
 K0 = 0.7978845608028654
@@ -51,9 +52,9 @@
     return h.astype(jnp.bfloat16), (dg * g).astype(jnp.bfloat16)
 
 
-def _kernel(x_h, g_ref, w1_h, w2_h, dy_h, y_h, dx_h, dw1_h, dw2_h, tl_h, W, dg_ref,
-            T, wo, wb, yacc, wacc, wt, xb, ob, dgb,
-            w1n, lsem, osem, bsem, tsend, trecv, wsend, wrecv, dgs, dgr):
+def _kernel(x_h, g_ref, w1_h, w2_h, dy_h, y_h, dx_h, dw1_h, dw2_h, tl_h, W, dg_h, w1t_h,
+            T, wo, wb, yacc, wacc, xb, ob, dgb, dgs8, dgo,
+            w1n, lsem, osem, bsem, tsend, trecv, wsend, wrecv, dgs):
     d = lax.axis_index("data")
     t = lax.axis_index("tp")
     z = t // 2
@@ -65,7 +66,7 @@
     dxn = lax.rem(d + 2, 4)
     dyn = d + 1 - 2 * lax.rem(d, 2)
     ddg = 3 - d
-    side = ((dxn, 3), (dyn, 4), (ddg, 5))
+    side = (dxn, dyn, ddg)
 
     def tslot(src, lane, h):
         return T.at[src, :, h, lane]
@@ -73,19 +74,25 @@
     def tcopy(src, lane, h, path, dev):
         s = tslot(src, lane, h)
         return pltpu.make_async_remote_copy(
-            src_ref=s, dst_ref=s, send_sem=tsend.at[src, h, path],
+            src_ref=s, dst_ref=s, send_sem=tsend.at[src, path],
             recv_sem=trecv.at[src, lane, h], device_id=dev, device_id_type=MESH)
 
-    def wcopy(src, lane, q, path, dev):
-        s = W.at[src, :, pl.ds(pl.multiple_of(lane * FF + q * (FF // 4), 32), FF // 4), :]
+    def tsent(src, path):
+        s = T.at[src, :, :, c]
+        pltpu.make_async_remote_copy(
+            src_ref=s, dst_ref=s, send_sem=tsend.at[src, path],
+            recv_sem=trecv.at[src, c, 0], device_id=partner, device_id_type=MESH).wait_send()
+
+    def wcopy(src, lane, q, path, dev, n=1):
+        s = W.at[src, :, pl.ds(pl.multiple_of(lane * FF + q * (FF // 4), 32), n * (FF // 4)), :]
         return pltpu.make_async_remote_copy(
-            src_ref=s, dst_ref=s, send_sem=wsend.at[src, q, path],
-            recv_sem=wrecv.at[src, lane, q], device_id=dev, device_id_type=MESH)
+            src_ref=s, dst_ref=s, send_sem=wsend.at[src, path],
+            recv_sem=wrecv.at[src, (0, 0, 1, 2)[path]], device_id=dev, device_id_type=MESH)
 
     def wown(lane):
         return pltpu.make_async_remote_copy(
-            src_ref=wo, dst_ref=W.at[z, :, pl.ds(pl.multiple_of(lane * FF, FF), FF), :], send_sem=wsend.at[z, 0, 2],
-            recv_sem=wrecv.at[z, lane, 0], device_id=partner, device_id_type=MESH)
+            src_ref=wo, dst_ref=W.at[z, :, pl.ds(pl.multiple_of(lane * FF, FF), FF), :], send_sem=wsend.at[z, 2],
+            recv_sem=wrecv.at[z, 1], device_id=partner, device_id_type=MESH)
 
     frow = pl.ds(pl.multiple_of(c * FF, FF), FF)
     l1 = pltpu.make_async_copy(w1_h, w1n, lsem.at[0])
@@ -101,7 +108,7 @@
     barrier = pltpu.get_barrier_semaphore()
     for k in range(1, 8):
         pl.semaphore_signal(barrier, inc=1, device_id=(d, lax.rem(t + k, 8)), device_id_type=MESH)
-    for dd, _p in side:
+    for dd in side:
         pl.semaphore_signal(barrier, inc=1, device_id=(dd, t), device_id_type=MESH)
     pl.semaphore_wait(barrier, 10)
 
@@ -109,8 +116,8 @@
         q = pl.ds(pl.multiple_of(d * (FF // 4), 32), FF // 4)
         return pltpu.make_async_remote_copy(
             src_ref=w2_h.at[q, :] if mat else wo.at[0, q, :],
-            dst_ref=W.at[z, mat, pl.ds(pl.multiple_of(c * FF + d * (FF // 4), 32), FF // 4), :], send_sem=wsend.at[z, d, path],
-            recv_sem=wrecv.at[z, c, d], device_id=dev, device_id_type=MESH)
+            dst_ref=W.at[z, mat, pl.ds(pl.multiple_of(c * FF + d * (FF // 4), 32), FF // 4), :], send_sem=wsend.at[z, path],
+            recv_sem=wrecv.at[z, 0], device_id=dev, device_id_type=MESH)
 
     @pl.when(z < 3)
     def _():
@@ -188,8 +195,8 @@
                 def _():
                     wcopy(src, c, d, 0, (d, 2 * (z - sgn) + c)).start()
 
-                for dd, path in side:
-                    wcopy(src, c, d, path, (dd, t)).start()
+                for dd in side:
+                    wcopy(src, c, d, 3, (dd, t)).start()
                 wcopy(src, c, d, 2, partner).start()
 
     def block(l1, l2, r1, r2, acc):
@@ -217,7 +224,7 @@
             town(NH // 2, NH)
 
         def epilogue():
-            dgb[t] = jnp.zeros((8, D), jnp.float32)
+            dgs8[...] = jnp.zeros((8, D), jnp.float32)
 
             @pl.loop(0, TOK // RT)
             def _(i):
@@ -226,7 +233,7 @@
                 xh, rstd = _ln(x)
                 dxn_ = yacc[0, r, :]
                 p = dxn_ * xh
-                dgb[t] += jnp.sum(p.reshape(RT // 8, 8, D), axis=0)
+                dgs8[...] += jnp.sum(p.reshape(RT // 8, 8, D), axis=0)
                 dxh = dxn_ * g_ref[...].reshape(1, D)
                 m1 = jnp.mean(dxh, axis=-1, keepdims=True)
                 m2 = jnp.mean(dxh * xh, axis=-1, keepdims=True)
@@ -236,20 +243,20 @@
                 ob[r, :] = (dyv + rstd * (dxh - m1 - xh * m2)).astype(jnp.bfloat16)
                 xb[r, :] = yacc[1, r, :].astype(jnp.bfloat16)
 
+            dgb[t] = jnp.sum(dgs8[...], axis=0, keepdims=True)
             pltpu.make_async_copy(xb, y_h, osem.at[0]).start()
             pltpu.make_async_copy(ob, dx_h, osem.at[1]).start()
             for k in range(1, 8):
                 pltpu.make_async_remote_copy(
-                    src_ref=dgb.at[t], dst_ref=dgb.at[t], send_sem=dgs.at[k],
-                    recv_sem=dgr.at[k], device_id=(d, lax.rem(t + k, 8)),
+                    src_ref=dgb.at[t], dst_ref=dgb.at[t], send_sem=dgs.at[0],
+                    recv_sem=dgs.at[1], device_id=(d, lax.rem(t + k, 8)),
                     device_id_type=MESH).start()
 
         def flush():
             with jax.named_scope("flush"):
                 pltpu.make_async_copy(wacc.at[1], dw2_h, osem.at[3]).start()
-                for i in range(FF // 128):
-                    wt[:, i * 128:(i + 1) * 128] = wacc[0, i * 128:(i + 1) * 128, :].T
-                pltpu.make_async_copy(wt, dw1_h, osem.at[2]).start()
+                pltpu.make_async_copy(wacc.at[0], dw1_h, osem.at[2]).start()
+                pltpu.make_async_copy(wo.at[0], w1t_h, osem.at[6]).start()
 
         def wpart():
             @pl.when(e == 0)
@@ -260,12 +267,11 @@
             @pl.when(e > 0)
             def _():
                 with jax.named_scope("wxywait"):
-                    for dd, _p in side:
-                        wcopy(src, c, dd, 2, partner).wait_recv()
+                    wcopy(src, c, 0, 3, partner, 3).wait_recv()
+                    for dd in side:
                         wcopy(src, c, dd, 2, partner).start()
                 with jax.named_scope("wd2dwait"):
-                    for q in range(4):
-                        wcopy(src, o, q, 2, partner).wait_recv()
+                    wcopy(src, o, 0, 2, partner, 4).wait_recv()
 
             with jax.named_scope("tokside"):
                 def fetch(i):
@@ -313,9 +319,7 @@
                 @pl.when(last)
                 def _():
                     with jax.named_scope("tlast"):
-                        cp = pltpu.make_async_copy(T.at[src, :, NH - 1], tl_h, osem.at[4])
-                        cp.start()
-                        cp.wait()
+                        pltpu.make_async_copy(T.at[src, :, NH - 1], tl_h, osem.at[4]).start()
 
                 @pl.when(jnp.logical_not(last))
                 def _():
@@ -323,32 +327,27 @@
                         block(wo[0], wo[1], T[src, 0, h].reshape(2 * TH, D),
                               T[src, 1, h].reshape(2 * TH, D), wacc)
 
-    for k in range(1, 8):
-        pltpu.make_async_remote_copy(
-            src_ref=dgb.at[t], dst_ref=dgb.at[t], send_sem=dgs.at[k],
-            recv_sem=dgr.at[k], device_id=partner, device_id_type=MESH).wait_recv()
-    dg_ref[...] = jnp.sum(jnp.sum(dgb[...], axis=0), axis=0)
-
-    for k in range(1, 8):
-        pltpu.make_async_remote_copy(
-            src_ref=dgb.at[t], dst_ref=dgb.at[t], send_sem=dgs.at[k],
-            recv_sem=dgr.at[k], device_id=partner, device_id_type=MESH).wait_send()
+    dgall = pltpu.make_async_remote_copy(
+        src_ref=dgb.at[pl.ds(0, 7)], dst_ref=dgb.at[pl.ds(0, 7)], send_sem=dgs.at[0],
+        recv_sem=dgs.at[1], device_id=partner, device_id_type=MESH)
+    dgall.wait_recv()
+    dgo[...] = jnp.sum(jnp.sum(dgb[...], axis=0), axis=0)
+    dgc = pltpu.make_async_copy(dgo, dg_h, osem.at[5])
+    dgc.start()
+
+    dgall.wait_send()
     wown(c).wait_send()
+    tsent(z, 2)
 
     @pl.when(z < 3)
     def _():
         wcopy(z, c, d, 0, up).wait_send()
-        for h in range(NH):
-            tcopy(z, c, h, 0, up).wait_send()
+        tsent(z, 0)
 
     @pl.when(z > 0)
     def _():
         wcopy(z, c, d, 1, down).wait_send()
-        for h in range(NH):
-            tcopy(z, c, h, 1, down).wait_send()
-
-    for h in range(NH):
-        tcopy(z, c, h, 2, partner).wait_send()
+        tsent(z, 1)
 
     @pl.loop(1, 7)
     def _(e):
@@ -362,37 +361,28 @@
             @pl.when((nxt >= 0) & (nxt <= 3))
             def _():
                 wcopy(src, c, d, 0, up).wait_send()
-                for h in range(NH):
-                    tcopy(src, c, h, 0, up).wait_send()
-
-            for dd, path in side:
-                wcopy(src, c, d, path, partner).wait_send()
-                wcopy(src, c, dd, 2, partner).wait_send()
-            wcopy(src, c, d, 2, partner).wait_send()
-            for h in range(NH):
-                tcopy(src, c, h, 2, partner).wait_send()
-
-    pltpu.make_async_copy(xb, y_h, osem.at[0]).wait()
-    pltpu.make_async_copy(ob, dx_h, osem.at[1]).wait()
+                tsent(src, 0)
+
+            wcopy(src, c, 0, 3, partner, 3).wait_send()
+            wcopy(src, c, 0, 2, partner, 4).wait_send()
+            tsent(src, 2)
+
     with jax.named_scope("owait"):
-        pltpu.make_async_copy(wt, dw1_h, osem.at[2]).wait()
+        pltpu.make_async_copy(xb, y_h, osem.at[0]).wait()
+        pltpu.make_async_copy(ob, dx_h, osem.at[1]).wait()
+        pltpu.make_async_copy(T.at[z, :, NH - 1], tl_h, osem.at[4]).wait()
+        dgc.wait()
+        pltpu.make_async_copy(wacc.at[0], dw1_h, osem.at[2]).wait()
+        pltpu.make_async_copy(wo.at[0], w1t_h, osem.at[6]).wait()
         pltpu.make_async_copy(wacc.at[1], dw2_h, osem.at[3]).wait()
 
 
 def _finish(tl_h, w1_h, w2_h, p1_h, p2_h, yp_h, dxp_h, dgp_h, y_h, dx_h, dw1_h, dw2_h, dg_h,
-            tl, w1, w2, a1, a2, yv, dxv, dgv, isem, osem):
+            tl, w1, w2, a1, a2, o1, yv, dxv, dgv, isem, osem):
     ins = [pltpu.make_async_copy(src, dst, isem.at[i]) for i, (src, dst) in enumerate(
         ((tl_h, tl), (w1_h, w1), (w2_h, w2), (p2_h, a2), (p1_h, a1), (yp_h, yv), (dxp_h, dxv), (dgp_h, dgv)))]
     for cp in ins:
         cp.start()
-    ins[0].wait()
-    xn = tl[0].reshape(2 * TH, D)
-    dy = tl[1].reshape(2 * TH, D)
-    ins[1].wait()
-    a = _nn(xn, w1[...])
-    ins[2].wait()
-    g = _nt(dy, w2[...])
-    h, da = _gelu_pair(a, g)
     outs = []
 
     def out(src, dst):
@@ -400,19 +390,32 @@
         cp.start()
         outs.append(cp)
 
-    for i, (src, dst) in ((5, (yv, y_h)), (6, (dxv, dx_h)), (7, (dgv, dg_h))):
-        ins[i].wait()
-        out(src, dst)
-    ins[3].wait()
-    for k in range(FF // 128):
-        r = slice(k * 128, (k + 1) * 128)
-        a2[r, :] += _tn(h[:, r], dy)
+    ins[0].wait()
+    xn = tl[0].reshape(2 * TH, D)
+    dy = tl[1].reshape(2 * TH, D)
+    for n, (r0, r1) in enumerate(STRIPS):
+        r = slice(r0, r1)
+        if n == 0:
+            ins[1].wait()
+        a = _nt(w1[r, :], xn)
+        if n == 0:
+            ins[2].wait()
+        g = _nt(w2[r, :], dy)
+        h, da = _gelu_pair(a, g)
+        if n == 0:
+            ins[3].wait()
+        a2[r, :] += _nn(h, dy)
         out(a2.at[r, :], dw2_h.at[r, :])
-    ins[4].wait()
-    for k in range(D // 256):
-        r = slice(k * 256, (k + 1) * 256)
-        a1[r, :] += _tn(xn[:, r], da)
-        out(a1.at[r, :], dw1_h.at[r, :])
+        if n == 0:
+            ins[4].wait()
+        a1[r, :] += _nn(da, xn)
+        for k in range(r0, r1, 128):
+            o1[:, k:k + 128] = a1[k:k + 128, :].T
+        out(o1.at[:, r], dw1_h.at[:, r])
+        if n == 0:
+            for i, (src, dst) in ((5, (yv, y_h)), (6, (dxv, dx_h)), (7, (dgv, dg_h))):
+                ins[i].wait()
+                out(src, dst)
     for cp in outs:
         cp.wait()
 
@@ -426,33 +429,33 @@
         vm = pl.BlockSpec(memory_space=pltpu.VMEM)
         sd = jax.ShapeDtypeStruct
         dma = pltpu.SemaphoreType.DMA
-        Yp, dXp, p1, p2, tl, _, dgp = pl.pallas_call(
+        Yp, dXp, p1, p2, tl, _, dgp, w1t = pl.pallas_call(
             _kernel,
             name="mlp_gather",
-            out_shape=(sd((TOK, D), bf), sd((TOK, D), bf), sd((D, FF), f32), sd((FF, D), f32),
-                       sd((2, 2, TH, D), bf), sd((4, 2, 2 * FF, D), bf), sd((D,), f32)),
+            out_shape=(sd((TOK, D), bf), sd((TOK, D), bf), sd((FF, D), f32), sd((FF, D), f32),
+                       sd((2, 2, TH, D), bf), sd((4, 2, 2 * FF, D), bf), sd((D,), f32), sd((FF, D), bf)),
             in_specs=[hbm, vm, hbm, hbm, hbm],
-            out_specs=[hbm] * 6 + [vm],
+            out_specs=[hbm] * 8,
             scratch_shapes=[
                 pltpu.VMEM((4, 2, NH, 2, TH, D), bf),
                 pltpu.VMEM((2, FF, D), bf),
                 pltpu.VMEM((2, 2, NB, D), bf),
                 pltpu.VMEM((2, TOK, D), f32),
                 pltpu.VMEM((2, FF, D), f32),
-                pltpu.VMEM((D, FF), f32),
                 pltpu.VMEM((TOK, D), bf),
                 pltpu.VMEM((TOK, D), bf),
-                pltpu.VMEM((8, 8, D), f32),
+                pltpu.VMEM((8, 1, D), f32),
+                pltpu.VMEM((8, D), f32),
+                pltpu.VMEM((D,), f32),
                 pltpu.VMEM((D, FF), bf),
                 dma((4 + NH,)),
-                dma((5,)),
+                dma((7,)),
                 dma((2,)),
-                dma((4, NH, 3)),
+                dma((4, 3)),
                 dma((4, 2, NH)),
-                dma((4, 4, 6)),
-                dma((4, 2, 4)),
-                dma((8,)),
-                dma((8,)),
+                dma((4, 4)),
+                dma((4, 3)),
+                dma((2,)),
             ],
             compiler_params=pltpu.CompilerParams(collective_id=0, has_side_effects=True, vmem_limit_bytes=VM1),
         )(X, gamma, W1, W2, dY)
@@ -464,18 +467,19 @@
             out_specs=[hbm] * 5,
             scratch_shapes=[
                 pltpu.VMEM((2, 2, TH, D), bf),
-                pltpu.VMEM((D, FF), bf),
                 pltpu.VMEM((FF, D), bf),
+                pltpu.VMEM((FF, D), bf),
+                pltpu.VMEM((FF, D), f32),
+                pltpu.VMEM((FF, D), f32),
                 pltpu.VMEM((D, FF), f32),
-                pltpu.VMEM((FF, D), f32),
                 pltpu.VMEM((TOK, D), bf),
                 pltpu.VMEM((TOK, D), bf),
                 pltpu.VMEM((D,), f32),
                 dma((8,)),
-                dma((13,)),
+                dma((3 + 2 * len(STRIPS),)),
             ],
             compiler_params=pltpu.CompilerParams(vmem_limit_bytes=VM2),
-        )(tl, W1, W2, p1, p2, Yp, dXp, dgp)
+        )(tl, w1t, W2, p1, p2, Yp, dXp, dgp)
 
     return jax.shard_map(body, mesh=mesh,
                          in_specs=(rows, P(None), P(None, "tp"), P("tp", None), rows),

time: 249 us -> 242 us (0.972)
  Pallas kernels: 248 us -> 241 us
    pallas_call x1, Pallas kernels: 240 us -> 233 us  [body(): pl.pallas_call(_kernel, name='mlp_gather', out_shape=(sd((TOK, D), bf), s...]
where the time goes in v3:
time: 242 us; the launch traced here: 241 us
  Pallas kernels  241 us (100%)
    pallas_call x1, Pallas kernels, body(): pl.pallas_call(_kernel, name='mlp_gather', out_shape=(sd((TOK, D), bf), s...  233 us
    pallas_call x1, Pallas kernels, body(): pl.pallas_call(_finish, name='mlp_finish', out_shape=(sd((TOK, D), bf), s...  8.06 us

profile of v3, /device:TPU:1, one launch (start us, length us, event | category | flops | bytes accessed | tf_op | source)
XLA Modules:
  0.0 241.4 jit_solution(13029492788809199066)
XLA Ops:
  0.6 232.7 %mlp_gather.1 = (bf16[512,1280]{1,0:T(8,128)(2,1)}, bf16[512,1280]{1,0:T(8,128)(2,1)}, f32[640,1280]{1,0:T(8,128)}, f32[640,1280]{1,0:T(8,128)}, bf16[2,2,128,12...) custom-call(bf16[512,1280]{1,0:T(8,128)(2,1)} %x_h.1, ...), custom_call_target="tpu_custom_call" | custom-call | tf_op jit(solution)/shard_map/mlp_gather/pallas_call | solution.py:432
  233.3 8.1 %mlp_finish.1 = (bf16[512,1280]{1,0:T(8,128)(2,1)}, bf16[512,1280]{1,0:T(8,128)(2,1)}, f32[1280,640]{1,0:T(8,128)}, f32[640,1280]{1,0:T(8,128)}, f32[1280]{0:T(1024)}) custom-call(bf16[2,2,128,1280]{3,2,1,0:T(8,128)(2,1)} %get-tuple-element.12.tl_h, bf16[640,1280]{1,0:T(8,128)(2,1)} %get-tuple-element.13.w1_h, bf16[640,1280]{1,0:T(8,128)(2,1)} %w2_h.3, ...), custom_call_target="tpu_custom_call" | custom-call | tf_op jit(solution)/shard_map/mlp_finish/pallas_call | solution.py:462

commit v4 on v3

--- a/solution.py
+++ b/solution.py
@@ -16,8 +16,8 @@
 NB = 256
 RT = 64
 STRIPS = ((0, 384), (384, 640))
-VM1 = 60 * 2**20
-VM2 = 60 * 2**20
+VM1 = 42 * 2**20
+VM2 = 20 * 2**20
 K0 = 0.7978845608028654
 K1 = 0.044715
 MESH = pl.DeviceIdType.MESH
@@ -52,9 +52,9 @@
     return h.astype(jnp.bfloat16), (dg * g).astype(jnp.bfloat16)
 
 
-def _kernel(x_h, g_ref, w1_h, w2_h, dy_h, y_h, dx_h, dw1_h, dw2_h, tl_h, W, dg_h, w1t_h,
-            T, wo, wb, yacc, wacc, xb, ob, dgb, dgs8, dgo,
-            w1n, lsem, osem, bsem, tsend, trecv, wsend, wrecv, dgs):
+def _kernel(x_h, g_h, w1_h, w2_h, dy_h, y_h, dx_h, p0, p1, p2, p3, p4, q0, q1, q2, q3, q4, tl_h, W, dg_h, w0_h, w1_o, w2_o, w3_h, w4_h,
+            T, wo, wb, yacc, wacc, g_ref, dgb, dgs8, dgo,
+            lsem, osem, bsem, tsend, trecv, wsend, wrecv, dgs):
     d = lax.axis_index("data")
     t = lax.axis_index("tp")
     z = t // 2
@@ -94,23 +94,36 @@
             src_ref=wo, dst_ref=W.at[z, :, pl.ds(pl.multiple_of(lane * FF, FF), FF), :], send_sem=wsend.at[z, 2],
             recv_sem=wrecv.at[z, 1], device_id=partner, device_id_type=MESH)
 
+    barrier = pltpu.get_barrier_semaphore()
+
+    def greet(dev):
+        pl.semaphore_signal(barrier, inc=1, device_id=dev, device_id_type=MESH)
+
+    pl.when(z < 3)(lambda: greet(up))
+    pl.when(z > 0)(lambda: greet(down))
+    greet(partner)
+    for dd in side:
+        greet((dd, t))
+
     frow = pl.ds(pl.multiple_of(c * FF, FF), FF)
-    l1 = pltpu.make_async_copy(w1_h, w1n, lsem.at[0])
+    w1b = [wb.at[i // 4, (i // 2) % 2, :, (i % 2) * FF:(i % 2 + 1) * FF] for i in range(D // NB)]
+    l1 = [pltpu.make_async_copy(w1_h.at[i * NB:(i + 1) * NB, :], w1b[i], lsem.at[4 + 2 * NH + i])
+          for i in range(D // NB)]
     l2 = pltpu.make_async_copy(w2_h, wo.at[1], lsem.at[1])
-    l3 = pltpu.make_async_copy(x_h, xb, lsem.at[2])
-    l1.start()
+    for cp in l1:
+        cp.start()
     l2.start()
-    l3.start()
+    l3 = [pltpu.make_async_copy(x_h.at[pl.ds(h * TH, TH), :], T.at[z, 0, h, c], lsem.at[4 + NH + h])
+          for h in range(NH)]
+    for cp in l3:
+        cp.start()
+    lg = pltpu.make_async_copy(g_h, g_ref, lsem.at[0])
+    lg.start()
     l4 = [pltpu.make_async_copy(dy_h.at[pl.ds(h * TH, TH), :], T.at[z, 1, h, c], lsem.at[3 + h])
           for h in range(NH)]
     for cp in l4:
         cp.start()
-    barrier = pltpu.get_barrier_semaphore()
-    for k in range(1, 8):
-        pl.semaphore_signal(barrier, inc=1, device_id=(d, lax.rem(t + k, 8)), device_id_type=MESH)
-    for dd in side:
-        pl.semaphore_signal(barrier, inc=1, device_id=(dd, t), device_id_type=MESH)
-    pl.semaphore_wait(barrier, 10)
+    pl.semaphore_wait(barrier, 4 + (z > 0).astype(jnp.int32) + (z < 3).astype(jnp.int32))
 
     def whalf(mat, path, dev):
         q = pl.ds(pl.multiple_of(d * (FF // 4), 32), FF // 4)
@@ -127,21 +140,22 @@
     def _():
         whalf(1, 1, down).start()
 
-    l1.wait()
-
-    for i in range(FF // 128):
-        wo[0, i * 128:(i + 1) * 128, :] = w1n[:, i * 128:(i + 1) * 128].T
+    for i in range(D // NB):
+        l1[i].wait()
+        wo[0, :, i * NB:(i + 1) * NB] = w1b[i][...].T
 
     l2.wait()
-    l3.wait()
+    lg.wait()
+    for cp in l3:
+        cp.wait()
 
     @pl.loop(0, TOK // RT)
     def _(i):
         r = pl.ds(pl.multiple_of(i * RT, RT), RT)
-        x = xb[r, :].astype(jnp.float32)
-        xh, _ = _ln(x)
         h = i // (TH // RT)
         rr = pl.ds(pl.multiple_of((i - h * (TH // RT)) * RT, RT), RT)
+        x = T[z, 0, h, c, rr, :].astype(jnp.float32)
+        xh, _ = _ln(x)
         T[z, 0, h, c, rr, :] = (xh * g_ref[...].reshape(1, D)).astype(jnp.bfloat16)
         yacc[1, r, :] = x
         yacc[0, r, :] = jnp.zeros((RT, D), jnp.float32)
@@ -223,13 +237,22 @@
         def _():
             town(NH // 2, NH)
 
+        def xcopy(n):
+            return pltpu.make_async_copy(x_h.at[n * NB:(n + 1) * NB, :], wb.at[0, n], bsem.at[n])
+
         def epilogue():
+            for n in range(2):
+                xcopy(n).start()
+            for n in range(2):
+                xcopy(n).wait()
             dgs8[...] = jnp.zeros((8, D), jnp.float32)
 
             @pl.loop(0, TOK // RT)
             def _(i):
                 r = pl.ds(pl.multiple_of(i * RT, RT), RT)
-                x = xb[r, :].astype(jnp.float32)
+                n = i // (NB // RT)
+                wr = pl.ds(pl.multiple_of((i - n * (NB // RT)) * RT, RT), RT)
+                x = wb[0, n, wr, :].astype(jnp.float32)
                 xh, rstd = _ln(x)
                 dxn_ = yacc[0, r, :]
                 p = dxn_ * xh
@@ -240,12 +263,13 @@
                 h = i // (TH // RT)
                 rr = pl.ds(pl.multiple_of((i - h * (TH // RT)) * RT, RT), RT)
                 dyv = T[z, 1, h, c, rr, :].astype(jnp.float32)
-                ob[r, :] = (dyv + rstd * (dxh - m1 - xh * m2)).astype(jnp.bfloat16)
-                xb[r, :] = yacc[1, r, :].astype(jnp.bfloat16)
+                wb[0, n, wr, :] = (dyv + rstd * (dxh - m1 - xh * m2)).astype(jnp.bfloat16)
+                wb[1, n, wr, :] = yacc[1, r, :].astype(jnp.bfloat16)
 
             dgb[t] = jnp.sum(dgs8[...], axis=0, keepdims=True)
-            pltpu.make_async_copy(xb, y_h, osem.at[0]).start()
-            pltpu.make_async_copy(ob, dx_h, osem.at[1]).start()
+            for n in range(2):
+                pltpu.make_async_copy(wb.at[1, n], y_h.at[n * NB:(n + 1) * NB, :], osem.at[2 * n]).start()
+                pltpu.make_async_copy(wb.at[0, n], dx_h.at[n * NB:(n + 1) * NB, :], osem.at[2 * n + 1]).start()
             for k in range(1, 8):
                 pltpu.make_async_remote_copy(
                     src_ref=dgb.at[t], dst_ref=dgb.at[t], send_sem=dgs.at[0],
@@ -254,9 +278,13 @@
 
         def flush():
             with jax.named_scope("flush"):
-                pltpu.make_async_copy(wacc.at[1], dw2_h, osem.at[3]).start()
-                pltpu.make_async_copy(wacc.at[0], dw1_h, osem.at[2]).start()
-                pltpu.make_async_copy(wo.at[0], w1t_h, osem.at[6]).start()
+                for i in range(5):
+                    pltpu.make_async_copy(wacc.at[1, i * 128:(i + 1) * 128, :], (q0, q1, q2, q3, q4)[i], osem.at[7]).start()
+                for i in range(5):
+                    pltpu.make_async_copy(wacc.at[0, i * 128:(i + 1) * 128, :], (p0, p1, p2, p3, p4)[i], osem.at[8]).start()
+                for i in range(5):
+                    pltpu.make_async_copy(wo.at[0, i * 128:(i + 1) * 128, :], (w0_h, w1_o, w2_o, w3_h, w4_h)[i],
+                                          osem.at[6]).start()
 
         def wpart():
             @pl.when(e == 0)
@@ -298,7 +326,7 @@
         def _():
             @pl.loop(0, NH)
             def _(h):
-                pl.when(h == NH // 2)(wpart)
+                pl.when(h == jnp.where(e == elast, 0, NH // 2))(wpart)
                 last = (e == elast) & (h == NH - 1)
                 pl.when(last)(flush)
 
@@ -368,21 +396,19 @@
             tsent(src, 2)
 
     with jax.named_scope("owait"):
-        pltpu.make_async_copy(xb, y_h, osem.at[0]).wait()
-        pltpu.make_async_copy(ob, dx_h, osem.at[1]).wait()
+        for n in range(2):
+            pltpu.make_async_copy(wb.at[1, n], y_h.at[n * NB:(n + 1) * NB, :], osem.at[2 * n]).wait()
+            pltpu.make_async_copy(wb.at[0, n], dx_h.at[n * NB:(n + 1) * NB, :], osem.at[2 * n + 1]).wait()
         pltpu.make_async_copy(T.at[z, :, NH - 1], tl_h, osem.at[4]).wait()
         dgc.wait()
-        pltpu.make_async_copy(wacc.at[0], dw1_h, osem.at[2]).wait()
-        pltpu.make_async_copy(wo.at[0], w1t_h, osem.at[6]).wait()
-        pltpu.make_async_copy(wacc.at[1], dw2_h, osem.at[3]).wait()
-
-
-def _finish(tl_h, w1_h, w2_h, p1_h, p2_h, yp_h, dxp_h, dgp_h, y_h, dx_h, dw1_h, dw2_h, dg_h,
-            tl, w1, w2, a1, a2, o1, yv, dxv, dgv, isem, osem):
-    ins = [pltpu.make_async_copy(src, dst, isem.at[i]) for i, (src, dst) in enumerate(
-        ((tl_h, tl), (w1_h, w1), (w2_h, w2), (p2_h, a2), (p1_h, a1), (yp_h, yv), (dxp_h, dxv), (dgp_h, dgv)))]
-    for cp in ins:
-        cp.start()
+        pltpu.make_async_copy(wacc.at[0], wacc.at[0], osem.at[8]).wait()
+        pltpu.make_async_copy(wo.at[0], wo.at[0], osem.at[6]).wait()
+        pltpu.make_async_copy(wacc.at[1], wacc.at[1], osem.at[7]).wait()
+
+
+def _finish(tl, w2, *refs):
+    p1, p2, w1 = refs[:5], refs[5:10], refs[10:15]
+    yv, dxv, dgv, y_h, dx_h, dw1_h, dw2_h, dg_h, o1, o2, osem = refs[15:]
     outs = []
 
     def out(src, dst):
@@ -390,32 +416,24 @@
         cp.start()
         outs.append(cp)
 
-    ins[0].wait()
+    out(yv, y_h)
+    out(dxv, dx_h)
+    out(dgv, dg_h)
     xn = tl[0].reshape(2 * TH, D)
     dy = tl[1].reshape(2 * TH, D)
-    for n, (r0, r1) in enumerate(STRIPS):
+    for r0, r1 in STRIPS:
         r = slice(r0, r1)
-        if n == 0:
-            ins[1].wait()
-        a = _nt(w1[r, :], xn)
-        if n == 0:
-            ins[2].wait()
+        a = _nt(jnp.concatenate([w1[k // 128][...] for k in range(r0, r1, 128)], axis=0), xn)
         g = _nt(w2[r, :], dy)
         h, da = _gelu_pair(a, g)
-        if n == 0:
-            ins[3].wait()
-        a2[r, :] += _nn(h, dy)
-        out(a2.at[r, :], dw2_h.at[r, :])
-        if n == 0:
-            ins[4].wait()
-        a1[r, :] += _nn(da, xn)
+        q = _nn(h, dy)
         for k in range(r0, r1, 128):
-            o1[:, k:k + 128] = a1[k:k + 128, :].T
+            o2[k:k + 128, :] = p2[k // 128][...] + q[k - r0:k - r0 + 128, :]
+        out(o2.at[r, :], dw2_h.at[r, :])
+        q = _nn(da, xn)
+        for k in range(r0, r1, 128):
+            o1[:, k:k + 128] = (p1[k // 128][...] + q[k - r0:k - r0 + 128, :]).T
         out(o1.at[:, r], dw1_h.at[:, r])
-        if n == 0:
-            for i, (src, dst) in ((5, (yv, y_h)), (6, (dxv, dx_h)), (7, (dgv, dg_h))):
-                ins[i].wait()
-                out(src, dst)
     for cp in outs:
         cp.wait()
 
@@ -429,27 +447,25 @@
         vm = pl.BlockSpec(memory_space=pltpu.VMEM)
         sd = jax.ShapeDtypeStruct
         dma = pltpu.SemaphoreType.DMA
-        Yp, dXp, p1, p2, tl, _, dgp, w1t = pl.pallas_call(
+        Yp, dXp, *pq = pl.pallas_call(
             _kernel,
             name="mlp_gather",
-            out_shape=(sd((TOK, D), bf), sd((TOK, D), bf), sd((FF, D), f32), sd((FF, D), f32),
-                       sd((2, 2, TH, D), bf), sd((4, 2, 2 * FF, D), bf), sd((D,), f32), sd((FF, D), bf)),
-            in_specs=[hbm, vm, hbm, hbm, hbm],
-            out_specs=[hbm] * 8,
+            out_shape=(sd((TOK, D), bf), sd((TOK, D), bf), *[sd((128, D), f32)] * 10,
+                       sd((2, 2, TH, D), bf), sd((4, 2, 2 * FF, D), bf), sd((D,), f32), *[sd((128, D), bf)] * 5),
+            in_specs=[hbm] * 5,
+            out_specs=[hbm] * 20,
             scratch_shapes=[
                 pltpu.VMEM((4, 2, NH, 2, TH, D), bf),
                 pltpu.VMEM((2, FF, D), bf),
                 pltpu.VMEM((2, 2, NB, D), bf),
                 pltpu.VMEM((2, TOK, D), f32),
                 pltpu.VMEM((2, FF, D), f32),
-                pltpu.VMEM((TOK, D), bf),
-                pltpu.VMEM((TOK, D), bf),
+                pltpu.VMEM((D,), f32),
                 pltpu.VMEM((8, 1, D), f32),
                 pltpu.VMEM((8, D), f32),
                 pltpu.VMEM((D,), f32),
-                pltpu.VMEM((D, FF), bf),
-                dma((4 + NH,)),
-                dma((7,)),
+                dma((4 + 2 * NH + D // NB,)),
+                dma((9,)),
                 dma((2,)),
                 dma((4, 3)),
                 dma((4, 2, NH)),
@@ -463,23 +479,15 @@
             _finish,
             name="mlp_finish",
             out_shape=(sd((TOK, D), bf), sd((TOK, D), bf), sd((D, FF), f32), sd((FF, D), f32), sd((D,), f32)),
-            in_specs=[hbm] * 8,
+            in_specs=[vm] * 20,
             out_specs=[hbm] * 5,
             scratch_shapes=[
-                pltpu.VMEM((2, 2, TH, D), bf),
-                pltpu.VMEM((FF, D), bf),
-                pltpu.VMEM((FF, D), bf),
+                pltpu.VMEM((D, FF), f32),
                 pltpu.VMEM((FF, D), f32),
-                pltpu.VMEM((FF, D), f32),
-                pltpu.VMEM((D, FF), f32),
-                pltpu.VMEM((TOK, D), bf),
-                pltpu.VMEM((TOK, D), bf),
-                pltpu.VMEM((D,), f32),
-                dma((8,)),
                 dma((3 + 2 * len(STRIPS),)),
             ],
             compiler_params=pltpu.CompilerParams(vmem_limit_bytes=VM2),
-        )(tl, w1t, W2, p1, p2, Yp, dXp, dgp)
+        )(pq[10], W2, *pq[:10], *pq[13:], Yp, dXp, pq[12])
 
     return jax.shard_map(body, mesh=mesh,
                          in_specs=(rows, P(None), P(None, "tp"), P("tp", None), rows),

time: 242 us -> 237 us (0.979)
  Pallas kernels: 241 us -> 235 us
    pallas_call x1, Pallas kernels: 8.06 us -> 4.8 us  [body(): pl.pallas_call(_finish, name='mlp_finish', out_shape=(sd((TOK, D), bf), s...]
where the time goes in v4:
time: 237 us
  Pallas kernels  235 us (99%)
    pallas_call x1, Pallas kernels, body(): pl.pallas_call(_kernel, name='mlp_gather', out_shape=(sd((TOK, D), bf), s...  231 us
    pallas_call x1, Pallas kernels, body(): pl.pallas_call(_finish, name='mlp_finish', out_shape=(sd((TOK, D), bf), s...  4.8 us

profile of v4, /device:TPU:1, one launch (start us, length us, event | category | flops | bytes accessed | tf_op | source)
XLA Modules:
  0.0 236.9 jit_solution(12988215966094742811)
XLA Ops:
  0.6 0.0 copy-start
  0.6 0.0 copy-start.1
  0.7 0.8 copy-done.1
  1.5 230.6 %mlp_gather.1 = (bf16[512,1280]{1,0:T(8,128)(2,1)S(1)}, bf16[512,1280]{1,0:T(8,128)(2,1)S(1)}, f32[128,1280]{1,0:T(8,128)S(1)}, f32[128,1280]{1,0:T(8,128)S(1)},...) custom-call(bf16[512,1280]{1,0:T(8,128)(2,1)} %x_h.1, ...), custom_call_target="tpu_custom_call" | custom-call | tf_op jit(solution)/shard_map/mlp_gather/pallas_call | solution.py:450
  232.1 0.0 copy-done
  232.1 4.8 %mlp_finish.1 = (bf16[512,1280]{1,0:T(8,128)(2,1)}, bf16[512,1280]{1,0:T(8,128)(2,1)}, f32[1280,640]{1,0:T(8,128)}, f32[640,1280]{1,0:T(8,128)}, f32[1280]{0:T(1024)}) custom-call(bf16[2,2,128,1280]{3,2,1,0:T(8,128)(2,1)S(1)} %get-tuple-element.24.tl, bf16[640,1280]{1,0:T(8,128)(2,1)S(1)} %copy-done, f32[128,1280]{1,0:T(8,128)S(1)} %get-tuple-element.25.refs_0_, ...), custom_call_target="tpu_custom_call" | custom-call | tf_op jit(solution)/shard_map/mlp_finish/pallas_call | solution.py:478
Async XLA Ops:
  0.6 231.4 %copy-start = (bf16[640,1280]{1,0:T(8,128)(2,1)S(1)}, bf16[640,1280]{1,0:T(8,128)(2,1)}, u32[]{:S(2)}) copy-start(bf16[640,1280]{1,0:T(8,128)(2,1)} %w2.1) | copy-start | bytes 4915204
  0.6 0.8 copy-start.1

commit v5 on v4

--- a/solution.py
+++ b/solution.py
@@ -15,7 +15,7 @@
 TH = TOK // NH
 NB = 256
 RT = 64
-STRIPS = ((0, 384), (384, 640))
+STRIPS = ((0, 256), (256, 512), (512, 640))
 VM1 = 42 * 2**20
 VM2 = 20 * 2**20
 K0 = 0.7978845608028654
@@ -474,7 +474,7 @@
                 dma((2,)),
             ],
             compiler_params=pltpu.CompilerParams(collective_id=0, has_side_effects=True, vmem_limit_bytes=VM1),
-        )(X, gamma, W1, W2, dY)
+        )(*(pltpu.with_memory_space_constraint(v, pltpu.HBM) for v in (X, gamma, W1, W2, dY)))
         return pl.pallas_call(
             _finish,
             name="mlp_finish",

time: 237 us -> 236 us (level)
  no operation moved by 1% of the time
where the time goes in v5:
time: 236 us
  Pallas kernels  235 us (100%)
    pallas_call x1, Pallas kernels, body(): pl.pallas_call(_kernel, name='mlp_gather', out_shape=(sd((TOK, D), bf), s...  231 us

profile of v5, /device:TPU:1, one launch (start us, length us, event | category | flops | bytes accessed | tf_op | source)
XLA Modules:
  0.0 235.6 jit_solution(13302808892915002821)
XLA Ops:
  0.6 0.0 copy-start
  0.6 230.7 %mlp_gather.1 = (bf16[512,1280]{1,0:T(8,128)(2,1)S(1)}, bf16[512,1280]{1,0:T(8,128)(2,1)S(1)}, f32[128,1280]{1,0:T(8,128)S(1)}, f32[128,1280]{1,0:T(8,128)S(1)},...) custom-call(bf16[512,1280]{1,0:T(8,128)(2,1)} %x_h.1, ...), custom_call_target="tpu_custom_call" | custom-call | tf_op jit(solution)/shard_map/mlp_gather/pallas_call | solution.py:450
  231.4 0.0 copy-done
  231.4 4.2 %mlp_finish.1 = (bf16[512,1280]{1,0:T(8,128)(2,1)}, bf16[512,1280]{1,0:T(8,128)(2,1)}, f32[1280,640]{1,0:T(8,128)}, f32[640,1280]{1,0:T(8,128)}, f32[1280]{0:T(1024)}) custom-call(bf16[2,2,128,1280]{3,2,1,0:T(8,128)(2,1)S(1)} %get-tuple-element.24.tl, bf16[640,1280]{1,0:T(8,128)(2,1)S(1)} %copy-done, f32[128,1280]{1,0:T(8,128)S(1)} %get-tuple-element.25.refs_0_, ...), custom_call_target="tpu_custom_call" | custom-call | tf_op jit(solution)/shard_map/mlp_finish/pallas_call | solution.py:478
Async XLA Ops:
  0.6 230.7 %copy-start = (bf16[640,1280]{1,0:T(8,128)(2,1)S(1)}, bf16[640,1280]{1,0:T(8,128)(2,1)}, u32[]{:S(2)}) copy-start(bf16[640,1280]{1,0:T(8,128)(2,1)} %w2.1) | copy-start | bytes 4915204

commit v6 on v5

--- a/solution.py
+++ b/solution.py
@@ -66,7 +66,6 @@
     dxn = lax.rem(d + 2, 4)
     dyn = d + 1 - 2 * lax.rem(d, 2)
     ddg = 3 - d
-    side = (dxn, dyn, ddg)
 
     def tslot(src, lane, h):
         return T.at[src, :, h, lane]
@@ -87,7 +86,7 @@
         s = W.at[src, :, pl.ds(pl.multiple_of(lane * FF + q * (FF // 4), 32), n * (FF // 4)), :]
         return pltpu.make_async_remote_copy(
             src_ref=s, dst_ref=s, send_sem=wsend.at[src, path],
-            recv_sem=wrecv.at[src, (0, 0, 1, 2)[path]], device_id=dev, device_id_type=MESH)
+            recv_sem=wrecv.at[src, (0, 0, 1, 2, 3)[path]], device_id=dev, device_id_type=MESH)
 
     def wown(lane):
         return pltpu.make_async_remote_copy(
@@ -102,7 +101,7 @@
     pl.when(z < 3)(lambda: greet(up))
     pl.when(z > 0)(lambda: greet(down))
     greet(partner)
-    for dd in side:
+    for dd in (dxn, dyn):
         greet((dd, t))
 
     frow = pl.ds(pl.multiple_of(c * FF, FF), FF)
@@ -123,7 +122,7 @@
           for h in range(NH)]
     for cp in l4:
         cp.start()
-    pl.semaphore_wait(barrier, 4 + (z > 0).astype(jnp.int32) + (z < 3).astype(jnp.int32))
+    pl.semaphore_wait(barrier, 3 + (z > 0).astype(jnp.int32) + (z < 3).astype(jnp.int32))
 
     def whalf(mat, path, dev):
         q = pl.ds(pl.multiple_of(d * (FF // 4), 32), FF // 4)
@@ -209,8 +208,13 @@
                 def _():
                     wcopy(src, c, d, 0, (d, 2 * (z - sgn) + c)).start()
 
-                for dd in side:
+                for dd in (dxn, dyn):
                     wcopy(src, c, d, 3, (dd, t)).start()
+
+                @pl.when(s > 1)
+                def _():
+                    wcopy(src, c, d, 4, (ddg, t)).start()
+
                 wcopy(src, c, d, 2, partner).start()
 
     def block(l1, l2, r1, r2, acc):
@@ -236,6 +240,12 @@
         @pl.when(e == 0)
         def _():
             town(NH // 2, NH)
+
+        def wside(src):
+            with jax.named_scope("wxywait"):
+                wcopy(src, c, 0, 3, partner, 2).wait_recv()
+                for dd in (dxn, dyn):
+                    wcopy(src, c, dd, 2, partner).start()
 
         def xcopy(n):
             return pltpu.make_async_copy(x_h.at[n * NB:(n + 1) * NB, :], wb.at[0, n], bsem.at[n])
@@ -294,10 +304,10 @@
 
             @pl.when(e > 0)
             def _():
-                with jax.named_scope("wxywait"):
-                    wcopy(src, c, 0, 3, partner, 3).wait_recv()
-                    for dd in side:
-                        wcopy(src, c, dd, 2, partner).start()
+                pl.when(s > 1)(lambda: wside(src))
+                with jax.named_scope("wdgwait"):
+                    wcopy(src, c, 0, 4, partner).wait_recv()
+                    wcopy(src, c, ddg, 2, partner).start()
                 with jax.named_scope("wd2dwait"):
                     wcopy(src, o, 0, 2, partner, 4).wait_recv()
 
@@ -354,6 +364,16 @@
                     with jax.named_scope("fside"):
                         block(wo[0], wo[1], T[src, 0, h].reshape(2 * TH, D),
                               T[src, 1, h].reshape(2 * TH, D), wacc)
+
+        @pl.when(e == 0)
+        def _():
+            for sg in (-1, 1):
+                near = z + sg
+
+                @pl.when((near >= 0) & (near <= 3))
+                def _():
+                    wside(near)
+                    wcopy(near, c, d, 4, (ddg, t)).start()
 
     dgall = pltpu.make_async_remote_copy(
         src_ref=dgb.at[pl.ds(0, 7)], dst_ref=dgb.at[pl.ds(0, 7)], send_sem=dgs.at[0],
@@ -391,7 +411,8 @@
                 wcopy(src, c, d, 0, up).wait_send()
                 tsent(src, 0)
 
-            wcopy(src, c, 0, 3, partner, 3).wait_send()
+            wcopy(src, c, 0, 3, partner, 2).wait_send()
+            wcopy(src, c, 0, 4, partner).wait_send()
             wcopy(src, c, 0, 2, partner, 4).wait_send()
             tsent(src, 2)
 
@@ -469,8 +490,8 @@
                 dma((2,)),
                 dma((4, 3)),
                 dma((4, 2, NH)),
+                dma((4, 5)),
                 dma((4, 4)),
-                dma((4, 3)),
                 dma((2,)),
             ],
             compiler_params=pltpu.CompilerParams(collective_id=0, has_side_effects=True, vmem_limit_bytes=VM1),

time: 236 us -> 235 us (level)
  no operation moved by 1% of the time
where the time goes in v6:
time: 235 us
  Pallas kernels  234 us (100%)
    pallas_call x1, Pallas kernels, body(): pl.pallas_call(_kernel, name='mlp_gather', out_shape=(sd((TOK, D), bf), s...  230 us

profile of v6, /device:TPU:1, one launch (start us, length us, event | category | flops | bytes accessed | tf_op | source)
XLA Modules:
  0.0 234.8 jit_solution(10470253267937920919)
XLA Ops:
  0.6 0.0 copy-start
  0.6 229.9 %mlp_gather.1 = (bf16[512,1280]{1,0:T(8,128)(2,1)S(1)}, bf16[512,1280]{1,0:T(8,128)(2,1)S(1)}, f32[128,1280]{1,0:T(8,128)S(1)}, f32[128,1280]{1,0:T(8,128)S(1)},...) custom-call(bf16[512,1280]{1,0:T(8,128)(2,1)} %x_h.1, ...), custom_call_target="tpu_custom_call" | custom-call | tf_op jit(solution)/shard_map/mlp_gather/pallas_call | solution.py:471
  230.5 0.0 copy-done
  230.5 4.2 %mlp_finish.1 = (bf16[512,1280]{1,0:T(8,128)(2,1)}, bf16[512,1280]{1,0:T(8,128)(2,1)}, f32[1280,640]{1,0:T(8,128)}, f32[640,1280]{1,0:T(8,128)}, f32[1280]{0:T(1024)}) custom-call(bf16[2,2,128,1280]{3,2,1,0:T(8,128)(2,1)S(1)} %get-tuple-element.24.tl, bf16[640,1280]{1,0:T(8,128)(2,1)S(1)} %copy-done, f32[128,1280]{1,0:T(8,128)S(1)} %get-tuple-element.25.refs_0_, ...), custom_call_target="tpu_custom_call" | custom-call | tf_op jit(solution)/shard_map/mlp_finish/pallas_call | solution.py:499
Async XLA Ops:
  0.6 229.9 %copy-start = (bf16[640,1280]{1,0:T(8,128)(2,1)S(1)}, bf16[640,1280]{1,0:T(8,128)(2,1)}, u32[]{:S(2)}) copy-start(bf16[640,1280]{1,0:T(8,128)(2,1)} %w2.1) | copy-start | bytes 4915204

commit v7 on v6

--- a/solution.py
+++ b/solution.py
@@ -106,19 +106,19 @@
 
     frow = pl.ds(pl.multiple_of(c * FF, FF), FF)
     w1b = [wb.at[i // 4, (i // 2) % 2, :, (i % 2) * FF:(i % 2 + 1) * FF] for i in range(D // NB)]
-    l1 = [pltpu.make_async_copy(w1_h.at[i * NB:(i + 1) * NB, :], w1b[i], lsem.at[4 + 2 * NH + i])
+    l1 = [pltpu.make_async_copy(w1_h.at[i * NB:(i + 1) * NB, :], w1b[i], lsem.at[2])
           for i in range(D // NB)]
     l2 = pltpu.make_async_copy(w2_h, wo.at[1], lsem.at[1])
     for cp in l1:
         cp.start()
     l2.start()
-    l3 = [pltpu.make_async_copy(x_h.at[pl.ds(h * TH, TH), :], T.at[z, 0, h, c], lsem.at[4 + NH + h])
+    l3 = [pltpu.make_async_copy(x_h.at[pl.ds(h * TH, TH), :], T.at[z, 0, h, c], lsem.at[3])
           for h in range(NH)]
     for cp in l3:
         cp.start()
     lg = pltpu.make_async_copy(g_h, g_ref, lsem.at[0])
     lg.start()
-    l4 = [pltpu.make_async_copy(dy_h.at[pl.ds(h * TH, TH), :], T.at[z, 1, h, c], lsem.at[3 + h])
+    l4 = [pltpu.make_async_copy(dy_h.at[pl.ds(h * TH, TH), :], T.at[z, 1, h, c], lsem.at[4])
           for h in range(NH)]
     for cp in l4:
         cp.start()
@@ -139,14 +139,13 @@
     def _():
         whalf(1, 1, down).start()
 
+    pltpu.make_async_copy(wo.at[0], wo.at[0], lsem.at[2]).wait()
     for i in range(D // NB):
-        l1[i].wait()
         wo[0, :, i * NB:(i + 1) * NB] = w1b[i][...].T
 
     l2.wait()
     lg.wait()
-    for cp in l3:
-        cp.wait()
+    pltpu.make_async_copy(T.at[z, 0, :, c], T.at[z, 0, :, c], lsem.at[3]).wait()
 
     @pl.loop(0, TOK // RT)
     def _(i):
@@ -168,7 +167,7 @@
         whalf(0, 1, down).start()
 
     wown(c).start()
-    lo = pltpu.make_async_copy(wo, W.at[z, :, frow, :], lsem.at[3 + NH])
+    lo = pltpu.make_async_copy(wo, W.at[z, :, frow, :], lsem.at[5])
     lo.start()
 
     @pl.loop(0, FF // RT)
@@ -177,8 +176,7 @@
         wacc[0, r, :] = jnp.zeros((RT, D), jnp.float32)
         wacc[1, r, :] = jnp.zeros((RT, D), jnp.float32)
 
-    for cp in l4:
-        cp.wait()
+    pltpu.make_async_copy(T.at[z, 1, :, c], T.at[z, 1, :, c], lsem.at[4]).wait()
 
     def town(h0, h1):
         @pl.when(z < 3)
@@ -246,6 +244,11 @@
                 wcopy(src, c, 0, 3, partner, 2).wait_recv()
                 for dd in (dxn, dyn):
                     wcopy(src, c, dd, 2, partner).start()
+
+        def dgpair(lane):
+            return pltpu.make_async_remote_copy(
+                src_ref=dgb.at[4 + lane], dst_ref=dgb.at[4 + lane], send_sem=dgs.at[2],
+                recv_sem=dgs.at[3], device_id=partner, device_id_type=MESH)
 
         def xcopy(n):
             return pltpu.make_async_copy(x_h.at[n * NB:(n + 1) * NB, :], wb.at[0, n], bsem.at[n])
@@ -276,14 +279,18 @@
                 wb[0, n, wr, :] = (dyv + rstd * (dxh - m1 - xh * m2)).astype(jnp.bfloat16)
                 wb[1, n, wr, :] = yacc[1, r, :].astype(jnp.bfloat16)
 
-            dgb[t] = jnp.sum(dgs8[...], axis=0, keepdims=True)
+            dgb[4 + c] = jnp.sum(dgs8[...], axis=0, keepdims=True)
             for n in range(2):
                 pltpu.make_async_copy(wb.at[1, n], y_h.at[n * NB:(n + 1) * NB, :], osem.at[2 * n]).start()
+            dgpair(c).start()
+            dgpair(o).wait_recv()
+            dgb[z] = dgb[4] + dgb[5]
+            for n in range(2):
                 pltpu.make_async_copy(wb.at[0, n], dx_h.at[n * NB:(n + 1) * NB, :], osem.at[2 * n + 1]).start()
-            for k in range(1, 8):
+            for k in range(1, 4):
                 pltpu.make_async_remote_copy(
-                    src_ref=dgb.at[t], dst_ref=dgb.at[t], send_sem=dgs.at[0],
-                    recv_sem=dgs.at[1], device_id=(d, lax.rem(t + k, 8)),
+                    src_ref=dgb.at[z], dst_ref=dgb.at[z], send_sem=dgs.at[0],
+                    recv_sem=dgs.at[1], device_id=(d, 2 * lax.rem(z + k, 4) + c),
                     device_id_type=MESH).start()
 
         def flush():
@@ -376,14 +383,17 @@
                     wcopy(near, c, d, 4, (ddg, t)).start()
 
     dgall = pltpu.make_async_remote_copy(
-        src_ref=dgb.at[pl.ds(0, 7)], dst_ref=dgb.at[pl.ds(0, 7)], send_sem=dgs.at[0],
+        src_ref=dgb.at[pl.ds(0, 3)], dst_ref=dgb.at[pl.ds(0, 3)], send_sem=dgs.at[0],
         recv_sem=dgs.at[1], device_id=partner, device_id_type=MESH)
     dgall.wait_recv()
-    dgo[...] = jnp.sum(jnp.sum(dgb[...], axis=0), axis=0)
+    dgo[...] = jnp.sum(jnp.sum(dgb[0:4], axis=0), axis=0)
     dgc = pltpu.make_async_copy(dgo, dg_h, osem.at[5])
     dgc.start()
 
     dgall.wait_send()
+    pltpu.make_async_remote_copy(
+        src_ref=dgb.at[4], dst_ref=dgb.at[4], send_sem=dgs.at[2],
+        recv_sem=dgs.at[3], device_id=partner, device_id_type=MESH).wait_send()
     wown(c).wait_send()
     tsent(z, 2)
 
@@ -485,14 +495,14 @@
                 pltpu.VMEM((8, 1, D), f32),
                 pltpu.VMEM((8, D), f32),
                 pltpu.VMEM((D,), f32),
-                dma((4 + 2 * NH + D // NB,)),
+                dma((6,)),
                 dma((9,)),
                 dma((2,)),
                 dma((4, 3)),
                 dma((4, 2, NH)),
                 dma((4, 5)),
                 dma((4, 4)),
-                dma((2,)),
+                dma((4,)),
             ],
             compiler_params=pltpu.CompilerParams(collective_id=0, has_side_effects=True, vmem_limit_bytes=VM1),
         )(*(pltpu.with_memory_space_constraint(v, pltpu.HBM) for v in (X, gamma, W1, W2, dY)))

time: 235 us -> 235 us (level)
  no operation moved by 1% of the time
where the time goes in v7:
time: 235 us; the launch traced here: 234 us
  Pallas kernels  234 us (100%)
    pallas_call x1, Pallas kernels, body(): pl.pallas_call(_kernel, name='mlp_gather', out_shape=(sd((TOK, D), bf), s...  229 us

profile of v7, /device:TPU:1, one launch (start us, length us, event | category | flops | bytes accessed | tf_op | source)
XLA Modules:
  0.0 234.3 jit_solution(7557208596883441010)
XLA Ops:
  0.6 0.0 copy-start
  0.6 229.5 %mlp_gather.1 = (bf16[512,1280]{1,0:T(8,128)(2,1)S(1)}, bf16[512,1280]{1,0:T(8,128)(2,1)S(1)}, f32[128,1280]{1,0:T(8,128)S(1)}, f32[128,1280]{1,0:T(8,128)S(1)},...) custom-call(bf16[512,1280]{1,0:T(8,128)(2,1)} %x_h.1, ...), custom_call_target="tpu_custom_call" | custom-call | tf_op jit(solution)/shard_map/mlp_gather/pallas_call | solution.py:481
  230.1 0.0 copy-done
  230.1 4.2 %mlp_finish.1 = (bf16[512,1280]{1,0:T(8,128)(2,1)}, bf16[512,1280]{1,0:T(8,128)(2,1)}, f32[1280,640]{1,0:T(8,128)}, f32[640,1280]{1,0:T(8,128)}, f32[1280]{0:T(1024)}) custom-call(bf16[2,2,128,1280]{3,2,1,0:T(8,128)(2,1)S(1)} %get-tuple-element.24.tl, bf16[640,1280]{1,0:T(8,128)(2,1)S(1)} %copy-done, f32[128,1280]{1,0:T(8,128)S(1)} %get-tuple-element.25.refs_0_, ...), custom_call_target="tpu_custom_call" | custom-call | tf_op jit(solution)/shard_map/mlp_finish/pallas_call | solution.py:509
Async XLA Ops:
  0.6 229.5 %copy-start = (bf16[640,1280]{1,0:T(8,128)(2,1)S(1)}, bf16[640,1280]{1,0:T(8,128)(2,1)}, u32[]{:S(2)}) copy-start(bf16[640,1280]{1,0:T(8,128)(2,1)} %w2.1) | copy-start | bytes 4915204
